TPU v7x, 128 devices: a whole 4x4x4 slice. The times are simulated.
128 devices in a mesh: gx: 8 (over z, core), gy: 2 (over x_lo), gz: 8 (over y, x_hi).
Axes of the slice: x: 4 (x_hi: 2, x_lo: 2; x = x_hi * 2 + x_lo), y: 4, z: 4, core: 2. Of those that a mesh axis runs over, the one named last changes fastest.
Arguments:
- amplitudes: float32 [2, 33554432], P(None, ('gx', 'gy', 'gz')), may hold values from -6 to 6
- couplings: float32 [25], replicated, may hold values from -1.2 to 1.2
- fields: float32 [25], replicated, may hold values from 0.3 to 1.2
Outputs:
- evolved: float32 [2, 33554432], P(None, ('gx', 'gy', 'gz'))
All inputs are finite; a program needn't handle non-finite values.
Results may differ from a plain program's by a relative error of at most 0.000098.
Values sent between devices are 32-bit elements; how exact they have to be, the bound alone decides.
No kernel may reach another device: no remote copies, remote signals or barrier semaphores. Data moves between devices by JAX's collectives and lax.ppermute only.
A program may use at most 64 MiB of HBM per device.

v0:
```python
import jax
import jax.numpy as jnp
from jax import lax
from jax.experimental import pallas as pl
from jax.experimental.pallas import tpu as pltpu
from jax.sharding import PartitionSpec as P


AXES = ("gx", "gy", "gz")
SIZES = (656, 672, 680, 688, 696, 704)
STARTS = tuple(sum(SIZES[:i]) for i in range(len(SIZES)))
F32 = jnp.float32
BF16 = jnp.bfloat16


def pair_table():
    place, table = {}, {}
    for gx in range(8):
        for gy in range(2):
            for gz in range(8):
                place[(gx >> 1, gx & 1, (gz & 1) * 2 + gy, gz >> 1)] = (gx * 2 + gy) * 8 + gz
    for (z, core, x, y), device in place.items():
        table[device] = {
            "core": core,
            "c": place[(z, core ^ 1, x, y)],
            "xA": place[(z, core, x ^ 1, y)],
            "xB": place[(z, core, x ^ 3, y)],
            "yA": place[(z, core, x, y ^ 1)],
            "yB": place[(z, core, x, y ^ 3)],
            "zA": place[(z ^ 1, core, x, y)],
            "zB": place[(z ^ 3, core, x, y)],
        }
    return table


def pairs_of(dim, first):
    table = pair_table()
    if dim == "c":
        return [(d, row["c"]) for d, row in table.items()]
    return [(d, row[dim + ("A" if (row["core"] == 0) == first else "B")]) for d, row in table.items()]


def spin(value, bit):
    return 1.0 - 2.0 * ((value >> bit) & 1).astype(F32)


def ones_in(value, bits):
    total = value & 1
    for bit in range(1, bits):
        total = total + ((value >> bit) & 1)
    return total


def turn(cosine, sine, quarter):
    quarter = quarter & 3
    odd = (quarter & 1) == 1
    real = jnp.where(odd, sine, cosine)
    imag = jnp.where(odd, cosine, -sine)
    sign = jnp.where(quarter >= 2, -1.0, 1.0)
    return real * sign, imag * sign


def split(value):
    high = value.astype(BF16)
    return high, (value - high.astype(F32)).astype(BF16)


def rotation(tangents, first, right):
    rows = lax.broadcasted_iota(jnp.int32, (128, 128), 0)
    cols = lax.broadcasted_iota(jnp.int32, (128, 128), 1)
    out_at, in_at = (cols, rows) if right else (rows, cols)
    differ = out_at ^ in_at
    result = jnp.ones((128, 128), F32)
    for bit in range(7):
        tangent = tangents[first + bit : first + bit + 1, :]
        signed = jnp.where(((out_at >> bit) & 1) == 1, tangent, -tangent)
        result = result * jnp.where(((differ >> bit) & 1) == 1, signed, 1.0)
    return result


def device_bits():
    number = (lax.axis_index("gx") * 2 + lax.axis_index("gy")) * 8 + lax.axis_index("gz")
    return number


def local_kernel(x_ref, j_ref, f_ref, *refs):
    outs, coef_ref, z_ref = refs[: len(SIZES)], refs[len(SIZES)], refs[len(SIZES) + 1]
    number = device_bits()
    bits = [(number >> k) & 1 for k in range(7)]
    sigma = [1.0 - 2.0 * b.astype(F32) for b in bits]
    row_at = lax.broadcasted_iota(jnp.int32, (32, 128), 0)
    angles = jnp.zeros((32, 128), F32)
    for q in range(25):
        angles = jnp.where(row_at == q, f_ref[q], angles)
    cosines = jnp.cos(angles)
    tangents = jnp.sin(angles) / cosines
    scale = cosines[0:1, :]
    for q in range(1, 25):
        scale = scale * cosines[q : q + 1, :]

    on_core0 = bits[4] == 0
    table = jnp.zeros((16, 128), F32)
    row16 = lax.broadcasted_iota(jnp.int32, (16, 128), 0)

    def put(table, row, value):
        return jnp.where(row16 == row, value, table)

    for k, (q0, q1) in enumerate(((21, 18), (19, 20), (23, 24))):
        s0 = -sigma[q0 - 18] * tangents[q0 : q0 + 1, :]
        s1 = -sigma[q1 - 18] * tangents[q1 : q1 + 1, :]
        both = s0 * s1
        table = put(table, 3 * k, jnp.where(on_core0, s0, both))
        table = put(table, 3 * k + 1, jnp.where(on_core0, both, -s0))
        table = put(table, 3 * k + 2, jnp.where(on_core0, -s1, s1))
    table = put(table, 9, -sigma[4] * tangents[22:23, :])
    coef_ref[...] = table

    low = lax.broadcasted_iota(jnp.int32, (16, 128), 0) * 128 + lax.broadcasted_iota(jnp.int32, (16, 128), 1)
    spins = [spin(low, q) for q in range(11)]
    phase = j_ref[24] * sigma[6] * spins[0]
    for q in range(10):
        phase = phase + j_ref[q] * (spins[q] * spins[q + 1])
    e1r, e1i = turn(jnp.cos(phase), jnp.sin(phase), ones_in(low, 11))
    high = lax.broadcasted_iota(jnp.int32, (8, 128), 1)
    spins = [spin(high, k) for k in range(7)]
    below = spin(lax.broadcasted_iota(jnp.int32, (8, 128), 0), 0)
    phase = j_ref[10] * (below * spins[0]) + (j_ref[17] * sigma[0]) * spins[6]
    for k in range(6):
        phase = phase + j_ref[11 + k] * (spins[k] * spins[k + 1])
    of_device = j_ref[18] * (sigma[0] * sigma[1])
    for k in range(1, 6):
        of_device = of_device + j_ref[18 + k] * (sigma[k] * sigma[k + 1])
    phase = phase + of_device
    device_ones = bits[0] + bits[1] + bits[2] + bits[3] + bits[4] + bits[5] + bits[6]
    e2r, e2i = turn(jnp.cos(phase), jnp.sin(phase), ones_in(high, 7) + device_ones)
    e2r, e2i = e2r * scale, e2i * scale

    lane_hi, lane_lo = split(rotation(tangents, 0, True))
    lane_mat = jnp.concatenate(
        [
            jnp.concatenate([lane_hi, lane_lo], axis=1),
            jnp.concatenate([lane_hi, jnp.zeros((128, 128), BF16)], axis=1),
        ],
        axis=0,
    )
    row_rot = rotation(tangents, 11, False)
    row_mats = []
    for v in range(2):
        mr, mi = row_rot * e2r[v : v + 1, :], row_rot * e2i[v : v + 1, :]
        row_mats.append(
            split(
                jnp.concatenate(
                    [jnp.concatenate([mr, -mi], axis=1), jnp.concatenate([mi, mr], axis=1)], axis=0
                )
            )
        )

    def lanes_done(rl):
        xre = x_ref[pl.ds(2 * rl, 128, stride=32), :]
        xim = x_ref[pl.ds(2 * rl + 1, 128, stride=32), :]
        er, ei = e1r[rl : rl + 1, :], e1i[rl : rl + 1, :]
        y = jnp.concatenate([xre * er - xim * ei, xre * ei + xim * er], axis=0)
        y_hi, y_lo = split(y)
        p = jnp.dot(jnp.concatenate([y_hi, y_lo], axis=1), lane_mat, preferred_element_type=F32)
        return p[:, :128] + p[:, 128:]

    for rl in range(0, 16, 2):
        m_hi, m_lo = row_mats[rl >> 3]
        y_hi, y_lo = split(jnp.concatenate([lanes_done(rl), lanes_done(rl + 1)], axis=1))
        z = jnp.dot(m_hi, y_hi, preferred_element_type=F32)
        z = z + jnp.dot(m_lo, y_hi, preferred_element_type=F32)
        z = z + jnp.dot(m_hi, y_lo, preferred_element_type=F32)
        z_ref[rl] = z[:, :128]
        z_ref[rl + 1] = z[:, 128:]

    low_tangents = [jnp.broadcast_to(tangents[7 + k : 8 + k, :], (8, 128)) for k in range(4)]
    for at in range(0, 256, 8):
        v = [z_ref[rl, at : at + 8, :] for rl in range(16)]
        for k in range(4):
            t = low_tangents[k]
            w = list(v)
            for rl in range(16):
                if rl >> k & 1:
                    w[rl] = v[rl] + t * v[rl ^ (1 << k)]
                else:
                    w[rl] = v[rl] - t * v[rl ^ (1 << k)]
            v = w
        for rl in range(16):
            row = rl * 256 + at
            s = max(i for i in range(len(SIZES)) if STARTS[i] <= row)
            outs[s][row - STARTS[s] : row - STARTS[s] + 8, :] = v[rl]


def final_kernel(*refs):
    ins, out_ref = refs[: len(SIZES)], refs[len(SIZES)]
    number = device_bits()
    device_ones = number & 1
    for k in range(1, 7):
        device_ones = device_ones + ((number >> k) & 1)
    rows = lax.broadcasted_iota(jnp.int32, (128, 128), 0)
    cols = lax.broadcasted_iota(jnp.int32, (128, 128), 1)
    base = ones_in(rows, 7) + ones_in(cols, 7) + device_ones

    def read(start):
        parts = []
        row = start
        while row < start + 128:
            s = max(i for i in range(len(SIZES)) if STARTS[i] <= row)
            stop = min(start + 128, STARTS[s] + SIZES[s])
            parts.append(ins[s][row - STARTS[s] : stop - STARTS[s], :])
            row = stop
        return parts[0] if len(parts) == 1 else jnp.concatenate(parts, axis=0)

    for rl in range(16):
        re, im = read(rl * 256), read(rl * 256 + 128)
        quarter = (base + bin(rl).count("1")) & 3
        odd = (quarter & 1) == 1
        out_re = jnp.where(odd, im, re)
        out_im = jnp.where(odd, re, im)
        out_ref[pl.ds(2 * rl, 128, stride=32), :] = jnp.where(quarter >= 2, -out_re, out_re)
        out_ref[pl.ds(2 * rl + 1, 128, stride=32), :] = jnp.where(
            (quarter == 1) | (quarter == 2), -out_im, out_im
        )


def exchange_order():
    count = len(SIZES)
    half = count // 2
    order = [(i, 0) for i in range(half)] + [(i, "c") for i in range(half, count)] + [(i, 0) for i in range(half, count)]
    for step in range(1, 6):
        order += [(i, step) for i in range(count)]
    return order + [(i, "c") for i in range(half)]


def shards(amplitudes, couplings, fields):
    rows = amplitudes.reshape(2, 2048, 128).transpose(1, 0, 2).reshape(4096, 128)
    vmem = pl.BlockSpec(memory_space=pltpu.VMEM)
    smem = pl.BlockSpec(memory_space=pltpu.SMEM)
    made = pl.pallas_call(
        local_kernel,
        out_shape=[jax.ShapeDtypeStruct((s, 128), F32) for s in SIZES] + [jax.ShapeDtypeStruct((16, 128), F32)],
        in_specs=[vmem, smem, smem],
        out_specs=[vmem] * (len(SIZES) + 1),
        scratch_shapes=[pltpu.VMEM((16, 256, 128), F32)],
        name="local_step",
    )(rows, couplings, fields)
    streams, coef = list(made[:-1]), made[-1]

    count = len(streams)
    kept = [None] * count
    for i, step in exchange_order():
        if step == "c":
            got = lax.ppermute(streams[i], AXES, pairs_of("c", True))
            streams[i] = streams[i] + coef[9:10] * got
            continue
        first = step % 2 == 0
        k = (step // 2 + i) % 3
        got = lax.ppermute(streams[i], AXES, pairs_of("xyz"[k], first))
        if first:
            mine = streams[i]
            kept[i] = mine + coef[3 * k : 3 * k + 1] * got
            streams[i] = coef[3 * k + 1 : 3 * k + 2] * mine + coef[3 * k + 2 : 3 * k + 3] * got
        else:
            streams[i] = kept[i] + got
    out = pl.pallas_call(
        final_kernel,
        out_shape=jax.ShapeDtypeStruct((4096, 128), F32),
        in_specs=[vmem] * count,
        out_specs=vmem,
        name="final_step",
    )(*streams)
    return out.reshape(2048, 2, 128).transpose(1, 0, 2).reshape(2, 262144)


def solution(mesh):
    placed = (P(None, AXES), P(), P())
    return jax.shard_map(shards, mesh=mesh, in_specs=placed, out_specs=P(None, AXES), check_vma=False)
```

profile of v0, /device:TPU:0, one launch (start us, length us, event | category | flops | bytes accessed | tf_op | source)
XLA Modules:
  0.0 108.1 jit_solution(3256065671690935381)
XLA Ops:
  0.0 6.5 %local_step.1 = (f32[656,128]{1,0:T(8,128)}, f32[672,128]{1,0:T(8,128)}, f32[680,128]{1,0:T(8,128)}, f32[688,128]{1,0:T(8,128)}, f32[696,128]{1,0:T(8,128)}, /*index=5*/f32[704,128]{1,0:T(8,128)}, f32[16,128]{1,0:T(8,128)}) custom-call(f32[4096,128]{1,0:T(8,128)} %bitcast.30, f32[25]{0:T(128)} %j_ref.1, f32[25]{0:T(128)} %f_ref.1), custom_call_target="tpu_custom_call" | custom-call | tf_op jit(solution)/shard_map/local_step/pallas_call | solution.py:239
  6.5 1.7 %collective-permute-start = (f32[656,128]{1,0:T(8,128)}, f32[656,128]{1,0:T(8,128)S(1)}, u32[]{:S(2)}, u32[]{:S(2)}) collective-permute-start(f32[656,128]{1,0:T(8,128)} %get-tuple-element.12), channel_id=1, source_target_pairs={{0,8},{1,9},{2,10},{3,11},{4,12},{5,13},{6,14},{7,15},{8,0},{9,1},... | collective-permute-start | bytes 1007624 | tf_op jit(solution)/shard_map/ppermute | solution.py:258
  8.2 1.6 %collective-permute-start.7 = (f32[672,128]{1,0:T(8,128)}, f32[672,128]{1,0:T(8,128)S(1)}, u32[]{:S(2)}, u32[]{:S(2)}) collective-permute-start(f32[672,128]{1,0:T(8,128)} %get-tuple-element.14), channel_id=1, source_target_pairs={{0,2},{1,3},{2,0},{3,1},{4,6},{5,7},{6,4},{7,5},{8,10},{9,11},{10,... | collective-permute-start | bytes 1032200 | tf_op jit(solution)/shard_map/ppermute | solution.py:258
  9.8 1.9 %collective-permute-start.14 = (f32[680,128]{1,0:T(8,128)}, f32[680,128]{1,0:T(8,128)S(1)}, u32[]{:S(2)}, u32[]{:S(2)}) collective-permute-start(f32[680,128]{1,0:T(8,128)} %get-tuple-element.15), channel_id=1, source_target_pairs={{0,32},{1,33},{2,34},{3,35},{4,36},{5,37},{6,38},{7,39},{8,40},{9,... | collective-permute-start | bytes 1044488 | tf_op jit(solution)/shard_map/ppermute | solution.py:258
  11.7 3.8 %collective-permute-start.21 = (f32[688,128]{1,0:T(8,128)}, f32[688,128]{1,0:T(8,128)S(1)}, u32[]{:S(2)}, u32[]{:S(2)}) collective-permute-start(f32[688,128]{1,0:T(8,128)} %get-tuple-element.16), channel_id=1, source_target_pairs={{0,16},{1,17},{2,18},{3,19},{4,20},{5,21},{6,22},{7,23},{8,24},{9,... | collective-permute-start | bytes 1056776 | tf_op jit(solution)/shard_map/ppermute | solution.py:253
  19.8 2.4 %collective-permute-start.8 = (f32[672,128]{1,0:T(8,128)S(1)}, f32[672,128]{1,0:T(8,128)S(1)}, u32[]{:S(2)}, u32[]{:S(2)}) collective-permute-start(f32[672,128]{1,0:T(8,128)S(1)} %multiply_add_fusion.19), channel_id=1, source_target_pairs={{0,6},{1,7},{2,4},{3,5},{4,2},{5,3},{6,0},{7,1},{8,14},{9,15},{10,... | collective-permute-start | bytes 1032200 | tf_op jit(solution)/shard_map/ppermute | solution.py:258
  22.2 4.1 %collective-permute-start.15 = (f32[680,128]{1,0:T(8,128)S(1)}, f32[680,128]{1,0:T(8,128)S(1)}, u32[]{:S(2)}, u32[]{:S(2)}) collective-permute-start(f32[680,128]{1,0:T(8,128)S(1)} %multiply_add_fusion.15), channel_id=1, source_target_pairs={{0,96},{1,97},{2,98},{3,99},{4,100},{5,101},{6,102},{7,103},{8,104... | collective-permute-start | bytes 1044488 | tf_op jit(solution)/shard_map/ppermute | solution.py:258
  29.6 4.7 %collective-permute-done.15 = f32[680,128]{1,0:T(8,128)S(1)} collective-permute-done((f32[680,128]{1,0:T(8,128)S(1)}, f32[680,128]{1,0:T(8,128)S(1)}, u32[]{:S(2)}, u32[]{:S(2)}) %collective-permute-start.15) | collective-permute-done | bytes 348192 | tf_op jit(solution)/shard_map/ppermute | solution.py:258
  35.7 1.6 %collective-permute-start.30 = (f32[696,128]{1,0:T(8,128)S(1)}, f32[696,128]{1,0:T(8,128)S(1)}, u32[]{:S(2)}, u32[]{:S(2)}) collective-permute-start(f32[696,128]{1,0:T(8,128)S(1)} %multiply_add_fusion.6), channel_id=1, source_target_pairs={{0,6},{1,7},{2,4},{3,5},{4,2},{5,3},{6,0},{7,1},{8,14},{9,15},{10,... | collective-permute-start | bytes 1069064 | tf_op jit(solution)/shard_map/ppermute | solution.py:258
  38.1 2.9 %collective-permute-start.37 = (f32[704,128]{1,0:T(8,128)S(1)}, f32[704,128]{1,0:T(8,128)S(1)}, u32[]{:S(2)}, u32[]{:S(2)}) collective-permute-start(f32[704,128]{1,0:T(8,128)S(1)} %multiply_add_fusion.2), channel_id=1, source_target_pairs={{0,96},{1,97},{2,98},{3,99},{4,100},{5,101},{6,102},{7,103},{8,104... | collective-permute-start | bytes 1081352 | tf_op jit(solution)/shard_map/ppermute | solution.py:258
  41.0 4.0 %collective-permute-done.9 = f32[672,128]{1,0:T(8,128)S(1)} collective-permute-done((f32[672,128]{1,0:T(8,128)S(1)}, f32[672,128]{1,0:T(8,128)S(1)}, u32[]{:S(2)}, u32[]{:S(2)}) %collective-permute-start.9) | collective-permute-done | bytes 344096 | tf_op jit(solution)/shard_map/ppermute | solution.py:258
  45.0 3.1 %collective-permute-start.3 = (f32[656,128]{1,0:T(8,128)S(1)}, f32[656,128]{1,0:T(8,128)S(1)}, u32[]{:S(2)}, u32[]{:S(2)}) collective-permute-start(f32[656,128]{1,0:T(8,128)S(1)} %multiply_add_fusion.22), channel_id=1, source_target_pairs={{0,6},{1,7},{2,4},{3,5},{4,2},{5,3},{6,0},{7,1},{8,14},{9,15},{10,... | collective-permute-start | bytes 1007624 | tf_op jit(solution)/shard_map/ppermute | solution.py:258
  50.3 3.2 %collective-permute-done.3 = f32[656,128]{1,0:T(8,128)S(1)} collective-permute-done((f32[656,128]{1,0:T(8,128)S(1)}, f32[656,128]{1,0:T(8,128)S(1)}, u32[]{:S(2)}, u32[]{:S(2)}) %collective-permute-start.3) | collective-permute-done | bytes 335904 | tf_op jit(solution)/shard_map/ppermute | solution.py:258
  53.6 1.7 %collective-permute-start.38 = (f32[704,128]{1,0:T(8,128)S(1)}, f32[704,128]{1,0:T(8,128)S(1)}, u32[]{:S(2)}, u32[]{:S(2)}) collective-permute-start(f32[704,128]{1,0:T(8,128)S(1)} %add_add_fusion.2), channel_id=1, source_target_pairs={{0,8},{1,9},{2,10},{3,11},{4,12},{5,13},{6,14},{7,15},{8,0},{9,1},... | collective-permute-start | bytes 1081352 | tf_op jit(solution)/shard_map/ppermute | solution.py:258
  55.3 5.1 %collective-permute-done.10 = f32[672,128]{1,0:T(8,128)S(1)} collective-permute-done((f32[672,128]{1,0:T(8,128)S(1)}, f32[672,128]{1,0:T(8,128)S(1)}, u32[]{:S(2)}, u32[]{:S(2)}) %collective-permute-start.10) | collective-permute-done | bytes 344096 | tf_op jit(solution)/shard_map/ppermute | solution.py:258
  61.9 5.8 %collective-permute-start.25 = (f32[688,128]{1,0:T(8,128)S(1)}, f32[688,128]{1,0:T(8,128)S(1)}, u32[]{:S(2)}, u32[]{:S(2)}) collective-permute-start(f32[688,128]{1,0:T(8,128)S(1)} %multiply_add_fusion.9), channel_id=1, source_target_pairs={{0,6},{1,7},{2,4},{3,5},{4,2},{5,3},{6,0},{7,1},{8,14},{9,15},{10,... | collective-permute-start | bytes 1056776 | tf_op jit(solution)/shard_map/ppermute | solution.py:258
  67.7 3.6 %collective-permute-start.32 = (f32[696,128]{1,0:T(8,128)S(1)}, f32[696,128]{1,0:T(8,128)S(1)}, u32[]{:S(2)}, u32[]{:S(2)}) collective-permute-start(f32[696,128]{1,0:T(8,128)S(1)} %multiply_add_fusion.5), channel_id=1, source_target_pairs={{0,96},{1,97},{2,98},{3,99},{4,100},{5,101},{6,102},{7,103},{8,104... | collective-permute-start | bytes 1069064 | tf_op jit(solution)/shard_map/ppermute | solution.py:258
  72.4 2.4 %collective-permute-start.5 = (f32[656,128]{1,0:T(8,128)S(1)}, f32[656,128]{1,0:T(8,128)S(1)}, u32[]{:S(2)}, u32[]{:S(2)}) collective-permute-start(f32[656,128]{1,0:T(8,128)S(1)} %multiply_add_fusion.21), channel_id=1, source_target_pairs={{0,96},{1,97},{2,98},{3,99},{4,100},{5,101},{6,102},{7,103},{8,104... | collective-permute-start | bytes 1007624 | tf_op jit(solution)/shard_map/ppermute | solution.py:258
  75.6 6.5 %collective-permute-start.19 = (f32[680,128]{1,0:T(8,128)S(1)}, f32[680,128]{1,0:T(8,128)S(1)}, u32[]{:S(2)}, u32[]{:S(2)}) collective-permute-start(f32[680,128]{1,0:T(8,128)S(1)} %multiply_add_fusion.13), channel_id=1, source_target_pairs={{0,6},{1,7},{2,4},{3,5},{4,2},{5,3},{6,0},{7,1},{8,14},{9,15},{10,... | collective-permute-start | bytes 1044488 | tf_op jit(solution)/shard_map/ppermute | solution.py:258
  82.9 2.7 %collective-permute-done.12 = f32[672,128]{1,0:T(8,128)S(1)} collective-permute-done((f32[672,128]{1,0:T(8,128)S(1)}, f32[672,128]{1,0:T(8,128)S(1)}, u32[]{:S(2)}, u32[]{:S(2)}) %collective-permute-start.12) | collective-permute-done | bytes 344096 | tf_op jit(solution)/shard_map/ppermute | solution.py:258
  85.6 1.7 %collective-permute-done.19 = f32[680,128]{1,0:T(8,128)S(1)} collective-permute-done((f32[680,128]{1,0:T(8,128)S(1)}, f32[680,128]{1,0:T(8,128)S(1)}, u32[]{:S(2)}, u32[]{:S(2)}) %collective-permute-start.19) | collective-permute-done | bytes 348192 | tf_op jit(solution)/shard_map/ppermute | solution.py:258
  87.4 2.2 %collective-permute-done.26 = f32[688,128]{1,0:T(8,128)S(1)} collective-permute-done((f32[688,128]{1,0:T(8,128)S(1)}, f32[688,128]{1,0:T(8,128)S(1)}, u32[]{:S(2)}, u32[]{:S(2)}) %collective-permute-start.26) | collective-permute-done | bytes 352288 | tf_op jit(solution)/shard_map/ppermute | solution.py:258
  92.1 4.7 %collective-permute-start.41 = (f32[704,128]{1,0:T(8,128)S(1)}, f32[704,128]{1,0:T(8,128)S(1)}, u32[]{:S(2)}, u32[]{:S(2)}) collective-permute-start(f32[704,128]{1,0:T(8,128)S(1)} %multiply_add_fusion), channel_id=1, source_target_pairs={{0,6},{1,7},{2,4},{3,5},{4,2},{5,3},{6,0},{7,1},{8,14},{9,15},{10,... | collective-permute-start | bytes 1081352 | tf_op jit(solution)/shard_map/ppermute | solution.py:258
  103.0 5.2 %final_step.1 = f32[4096,128]{1,0:T(8,128)} custom-call(f32[656,128]{1,0:T(8,128)} %multiply_add_fusion.20.refs_0_, f32[672,128]{1,0:T(8,128)} %multiply_add_fusion.16.refs_1_, f32[680,128]{1,0:T(8,128)} %multiply_add_fusion.12.refs_2_, f32[688,128]{1,0:T(8,128)} %add_add_fusion.6.refs_3_, f32[696,128]{1,0:T(8,128)} %add_add_fusion.3.refs_4_, ...), custom_call_target="tpu_custom_call" | custom-call | tf_op jit(solution)/shard_map/final_step/pallas_call | solution.py:265
  (117 shorter events, 24.6 us)
Async XLA Ops:
  11.7 10.5 %collective-permute-start.21 = (f32[688,128]{1,0:T(8,128)}, f32[688,128]{1,0:T(8,128)S(1)}, u32[]{:S(2)}, u32[]{:S(2)}) collective-permute-start(f32[688,128]{1,0:T(8,128)} %get-tuple-element.16), channel_id=1, source_target_pairs={{0,16},{1,17},{2,18},{3,19},{4,20},{5,21},{6,22},{7,23},{8,24},{9,... | collective-permute-start | bytes 1056776 | tf_op jit(solution)/shard_map/ppermute | solution.py:253
  15.5 10.8 %collective-permute-start.28 = (f32[696,128]{1,0:T(8,128)}, f32[696,128]{1,0:T(8,128)S(1)}, u32[]{:S(2)}, u32[]{:S(2)}) collective-permute-start(f32[696,128]{1,0:T(8,128)} %get-tuple-element.17), channel_id=1, source_target_pairs={{0,16},{1,17},{2,18},{3,19},{4,20},{5,21},{6,22},{7,23},{8,24},{9,... | collective-permute-start | bytes 1069064 | tf_op jit(solution)/shard_map/ppermute | solution.py:253
  16.5 10.4 %collective-permute-start.35 = (f32[704,128]{1,0:T(8,128)}, f32[704,128]{1,0:T(8,128)S(1)}, u32[]{:S(2)}, u32[]{:S(2)}) collective-permute-start(f32[704,128]{1,0:T(8,128)} %get-tuple-element.18), channel_id=1, source_target_pairs={{0,16},{1,17},{2,18},{3,19},{4,20},{5,21},{6,22},{7,23},{8,24},{9,... | collective-permute-start | bytes 1081352 | tf_op jit(solution)/shard_map/ppermute | solution.py:253
  22.2 12.1 %collective-permute-start.15 = (f32[680,128]{1,0:T(8,128)S(1)}, f32[680,128]{1,0:T(8,128)S(1)}, u32[]{:S(2)}, u32[]{:S(2)}) collective-permute-start(f32[680,128]{1,0:T(8,128)S(1)} %multiply_add_fusion.15), channel_id=1, source_target_pairs={{0,96},{1,97},{2,98},{3,99},{4,100},{5,101},{6,102},{7,103},{8,104... | collective-permute-start | bytes 1044488 | tf_op jit(solution)/shard_map/ppermute | solution.py:258
  34.3 10.7 %collective-permute-start.9 = (f32[672,128]{1,0:T(8,128)S(1)}, f32[672,128]{1,0:T(8,128)S(1)}, u32[]{:S(2)}, u32[]{:S(2)}) collective-permute-start(f32[672,128]{1,0:T(8,128)S(1)} %add_add_fusion.14), channel_id=1, source_target_pairs={{0,32},{1,33},{2,34},{3,35},{4,36},{5,37},{6,38},{7,39},{8,40},{9,... | collective-permute-start | bytes 1032200 | tf_op jit(solution)/shard_map/ppermute | solution.py:258
  34.4 13.8 %collective-permute-start.16 = (f32[680,128]{1,0:T(8,128)S(1)}, f32[680,128]{1,0:T(8,128)S(1)}, u32[]{:S(2)}, u32[]{:S(2)}) collective-permute-start(f32[680,128]{1,0:T(8,128)S(1)} %add_add_fusion.11), channel_id=1, source_target_pairs={{0,8},{1,9},{2,10},{3,11},{4,12},{5,13},{6,14},{7,15},{8,0},{9,1},... | collective-permute-start | bytes 1044488 | tf_op jit(solution)/shard_map/ppermute | solution.py:258
  34.8 14.4 %collective-permute-start.23 = (f32[688,128]{1,0:T(8,128)S(1)}, f32[688,128]{1,0:T(8,128)S(1)}, u32[]{:S(2)}, u32[]{:S(2)}) collective-permute-start(f32[688,128]{1,0:T(8,128)S(1)} %multiply_add_fusion.10), channel_id=1, source_target_pairs={{0,9},{1,8},{2,11},{3,10},{4,13},{5,12},{6,15},{7,14},{8,1},{9,0},... | collective-permute-start | bytes 1056776 | tf_op jit(solution)/shard_map/ppermute | solution.py:258
  35.7 14.3 %collective-permute-start.30 = (f32[696,128]{1,0:T(8,128)S(1)}, f32[696,128]{1,0:T(8,128)S(1)}, u32[]{:S(2)}, u32[]{:S(2)}) collective-permute-start(f32[696,128]{1,0:T(8,128)S(1)} %multiply_add_fusion.6), channel_id=1, source_target_pairs={{0,6},{1,7},{2,4},{3,5},{4,2},{5,3},{6,0},{7,1},{8,14},{9,15},{10,... | collective-permute-start | bytes 1069064 | tf_op jit(solution)/shard_map/ppermute | solution.py:258
  38.1 12.1 %collective-permute-start.37 = (f32[704,128]{1,0:T(8,128)S(1)}, f32[704,128]{1,0:T(8,128)S(1)}, u32[]{:S(2)}, u32[]{:S(2)}) collective-permute-start(f32[704,128]{1,0:T(8,128)S(1)} %multiply_add_fusion.2), channel_id=1, source_target_pairs={{0,96},{1,97},{2,98},{3,99},{4,100},{5,101},{6,102},{7,103},{8,104... | collective-permute-start | bytes 1081352 | tf_op jit(solution)/shard_map/ppermute | solution.py:258
  48.2 12.2 %collective-permute-start.10 = (f32[672,128]{1,0:T(8,128)S(1)}, f32[672,128]{1,0:T(8,128)S(1)}, u32[]{:S(2)}, u32[]{:S(2)}) collective-permute-start(f32[672,128]{1,0:T(8,128)S(1)} %multiply_add_fusion.18), channel_id=1, source_target_pairs={{0,96},{1,97},{2,98},{3,99},{4,100},{5,101},{6,102},{7,103},{8,104... | collective-permute-start | bytes 1032200 | tf_op jit(solution)/shard_map/ppermute | solution.py:258
  49.2 12.3 %collective-permute-start.17 = (f32[680,128]{1,0:T(8,128)S(1)}, f32[680,128]{1,0:T(8,128)S(1)}, u32[]{:S(2)}, u32[]{:S(2)}) collective-permute-start(f32[680,128]{1,0:T(8,128)S(1)} %multiply_add_fusion.14), channel_id=1, source_target_pairs={{0,9},{1,8},{2,11},{3,10},{4,13},{5,12},{6,15},{7,14},{8,1},{9,0},... | collective-permute-start | bytes 1044488 | tf_op jit(solution)/shard_map/ppermute | solution.py:258
  50.0 11.5 %collective-permute-start.24 = (f32[688,128]{1,0:T(8,128)S(1)}, f32[688,128]{1,0:T(8,128)S(1)}, u32[]{:S(2)}, u32[]{:S(2)}) collective-permute-start(f32[688,128]{1,0:T(8,128)S(1)} %add_add_fusion.8), channel_id=1, source_target_pairs={{0,2},{1,3},{2,0},{3,1},{4,6},{5,7},{6,4},{7,5},{8,10},{9,11},{10,... | collective-permute-start | bytes 1056776 | tf_op jit(solution)/shard_map/ppermute | solution.py:258
  50.2 11.7 %collective-permute-start.31 = (f32[696,128]{1,0:T(8,128)S(1)}, f32[696,128]{1,0:T(8,128)S(1)}, u32[]{:S(2)}, u32[]{:S(2)}) collective-permute-start(f32[696,128]{1,0:T(8,128)S(1)} %add_add_fusion.5), channel_id=1, source_target_pairs={{0,32},{1,33},{2,34},{3,35},{4,36},{5,37},{6,38},{7,39},{8,40},{9,... | collective-permute-start | bytes 1069064 | tf_op jit(solution)/shard_map/ppermute | solution.py:258
  53.6 14.2 %collective-permute-start.38 = (f32[704,128]{1,0:T(8,128)S(1)}, f32[704,128]{1,0:T(8,128)S(1)}, u32[]{:S(2)}, u32[]{:S(2)}) collective-permute-start(f32[704,128]{1,0:T(8,128)S(1)} %add_add_fusion.2), channel_id=1, source_target_pairs={{0,8},{1,9},{2,10},{3,11},{4,12},{5,13},{6,14},{7,15},{8,0},{9,1},... | collective-permute-start | bytes 1081352 | tf_op jit(solution)/shard_map/ppermute | solution.py:258
  60.4 10.9 %collective-permute-start.4 = (f32[656,128]{1,0:T(8,128)S(1)}, f32[656,128]{1,0:T(8,128)S(1)}, u32[]{:S(2)}, u32[]{:S(2)}) collective-permute-start(f32[656,128]{1,0:T(8,128)S(1)} %add_add_fusion.16), channel_id=1, source_target_pairs={{0,32},{1,33},{2,34},{3,35},{4,36},{5,37},{6,38},{7,39},{8,40},{9,... | collective-permute-start | bytes 1007624 | tf_op jit(solution)/shard_map/ppermute | solution.py:258
  61.5 10.9 %collective-permute-start.11 = (f32[672,128]{1,0:T(8,128)S(1)}, f32[672,128]{1,0:T(8,128)S(1)}, u32[]{:S(2)}, u32[]{:S(2)}) collective-permute-start(f32[672,128]{1,0:T(8,128)S(1)} %add_add_fusion.13), channel_id=1, source_target_pairs={{0,8},{1,9},{2,10},{3,11},{4,12},{5,13},{6,14},{7,15},{8,0},{9,1},... | collective-permute-start | bytes 1032200 | tf_op jit(solution)/shard_map/ppermute | solution.py:258
  61.6 13.3 %collective-permute-start.18 = (f32[680,128]{1,0:T(8,128)S(1)}, f32[680,128]{1,0:T(8,128)S(1)}, u32[]{:S(2)}, u32[]{:S(2)}) collective-permute-start(f32[680,128]{1,0:T(8,128)S(1)} %add_add_fusion.10), channel_id=1, source_target_pairs={{0,2},{1,3},{2,0},{3,1},{4,6},{5,7},{6,4},{7,5},{8,10},{9,11},{10,... | collective-permute-start | bytes 1044488 | tf_op jit(solution)/shard_map/ppermute | solution.py:258
  61.9 13.6 %collective-permute-start.25 = (f32[688,128]{1,0:T(8,128)S(1)}, f32[688,128]{1,0:T(8,128)S(1)}, u32[]{:S(2)}, u32[]{:S(2)}) collective-permute-start(f32[688,128]{1,0:T(8,128)S(1)} %multiply_add_fusion.9), channel_id=1, source_target_pairs={{0,6},{1,7},{2,4},{3,5},{4,2},{5,3},{6,0},{7,1},{8,14},{9,15},{10,... | collective-permute-start | bytes 1056776 | tf_op jit(solution)/shard_map/ppermute | solution.py:258
  67.7 14.4 %collective-permute-start.32 = (f32[696,128]{1,0:T(8,128)S(1)}, f32[696,128]{1,0:T(8,128)S(1)}, u32[]{:S(2)}, u32[]{:S(2)}) collective-permute-start(f32[696,128]{1,0:T(8,128)S(1)} %multiply_add_fusion.5), channel_id=1, source_target_pairs={{0,96},{1,97},{2,98},{3,99},{4,100},{5,101},{6,102},{7,103},{8,104... | collective-permute-start | bytes 1069064 | tf_op jit(solution)/shard_map/ppermute | solution.py:258
  71.4 10.9 %collective-permute-start.39 = (f32[704,128]{1,0:T(8,128)S(1)}, f32[704,128]{1,0:T(8,128)S(1)}, u32[]{:S(2)}, u32[]{:S(2)}) collective-permute-start(f32[704,128]{1,0:T(8,128)S(1)} %multiply_add_fusion.1), channel_id=1, source_target_pairs={{0,9},{1,8},{2,11},{3,10},{4,13},{5,12},{6,15},{7,14},{8,1},{9,0},... | collective-permute-start | bytes 1081352 | tf_op jit(solution)/shard_map/ppermute | solution.py:258
  72.4 10.4 %collective-permute-start.5 = (f32[656,128]{1,0:T(8,128)S(1)}, f32[656,128]{1,0:T(8,128)S(1)}, u32[]{:S(2)}, u32[]{:S(2)}) collective-permute-start(f32[656,128]{1,0:T(8,128)S(1)} %multiply_add_fusion.21), channel_id=1, source_target_pairs={{0,96},{1,97},{2,98},{3,99},{4,100},{5,101},{6,102},{7,103},{8,104... | collective-permute-start | bytes 1007624 | tf_op jit(solution)/shard_map/ppermute | solution.py:258
  74.9 10.7 %collective-permute-start.12 = (f32[672,128]{1,0:T(8,128)S(1)}, f32[672,128]{1,0:T(8,128)S(1)}, u32[]{:S(2)}, u32[]{:S(2)}) collective-permute-start(f32[672,128]{1,0:T(8,128)S(1)} %multiply_add_fusion.17), channel_id=1, source_target_pairs={{0,9},{1,8},{2,11},{3,10},{4,13},{5,12},{6,15},{7,14},{8,1},{9,0},... | collective-permute-start | bytes 1032200 | tf_op jit(solution)/shard_map/ppermute | solution.py:258
  75.6 11.7 %collective-permute-start.19 = (f32[680,128]{1,0:T(8,128)S(1)}, f32[680,128]{1,0:T(8,128)S(1)}, u32[]{:S(2)}, u32[]{:S(2)}) collective-permute-start(f32[680,128]{1,0:T(8,128)S(1)} %multiply_add_fusion.13), channel_id=1, source_target_pairs={{0,6},{1,7},{2,4},{3,5},{4,2},{5,3},{6,0},{7,1},{8,14},{9,15},{10,... | collective-permute-start | bytes 1044488 | tf_op jit(solution)/shard_map/ppermute | solution.py:258
  87.3 10.3 %collective-permute-start.13 = (f32[672,128]{1,0:T(8,128)S(1)}, f32[672,128]{1,0:T(8,128)S(1)}, u32[]{:S(2)}, u32[]{:S(2)}) collective-permute-start(f32[672,128]{1,0:T(8,128)S(1)} %add_add_fusion.12), channel_id=1, source_target_pairs={{0,16},{1,17},{2,18},{3,19},{4,20},{5,21},{6,22},{7,23},{8,24},{9,... | collective-permute-start | bytes 1032200 | tf_op jit(solution)/shard_map/ppermute | solution.py:253
  (24 other events, 230.3 us)
where the time goes:
time: 108 us
  starting transfers between devices  56.3 us (52%)
  waiting for transfers between devices  30.1 us (28%)
  Pallas kernels  11.7 us (11%)
  other arithmetic  8.68 us (8%)
    ppermute x36, starting transfers between devices, shards(): got = lax.ppermute(streams[i], AXES, pairs_of('xyz'[k], first))  51.9 us
    ppermute x36, waiting for transfers between devices, shards(): got = lax.ppermute(streams[i], AXES, pairs_of('xyz'[k], first))  30.1 us
    pallas_call x1, Pallas kernels, shards(): pl.pallas_call(local_kernel, out_shape=[jax.ShapeDtypeStruct((s, 128), F3...  6.5 us
    pallas_call x1, Pallas kernels, shards(): pl.pallas_call(final_kernel, out_shape=jax.ShapeDtypeStruct((4096, 128),...  5.15 us
    ppermute x6, starting transfers between devices, shards(): got = lax.ppermute(streams[i], AXES, pairs_of('c', True))  4.42 us
    add x18, other arithmetic, shards(): streams[i] = kept[i] + got  3.48 us
    add x18, other arithmetic, shards(): coef[3 * k + 1:3 * k + 2] * mine + coef[3 * k + 2:3 * k + 3] * got  2.74 us
    add x6, other arithmetic, shards(): streams[i] = streams[i] + coef[9:10] * got  2.46 us
  transfers between devices with their start and end apart: 42, of which 16 were waited for; matrix products, arithmetic and copies ran while one was open for 8% of the time, Pallas kernels for 0%

commit v1 on v0

--- a/solution.py
+++ b/solution.py
@@ -225,11 +225,7 @@
 
 def exchange_order():
     count = len(SIZES)
-    half = count // 2
-    order = [(i, 0) for i in range(half)] + [(i, "c") for i in range(half, count)] + [(i, 0) for i in range(half, count)]
-    for step in range(1, 6):
-        order += [(i, step) for i in range(count)]
-    return order + [(i, "c") for i in range(half)]
+    return [(i, step) for step in ("c", 0, 1, 2, 3, 4, 5) for i in range(count)]
 
 
 def shards(amplitudes, couplings, fields):
@@ -238,7 +234,7 @@
     smem = pl.BlockSpec(memory_space=pltpu.SMEM)
     made = pl.pallas_call(
         local_kernel,
-        out_shape=[jax.ShapeDtypeStruct((s, 128), F32) for s in SIZES] + [jax.ShapeDtypeStruct((16, 128), F32)],
+        out_shape=[pltpu.VMEM((s, 128), F32) for s in SIZES] + [pltpu.VMEM((16, 128), F32)],
         in_specs=[vmem, smem, smem],
         out_specs=[vmem] * (len(SIZES) + 1),
         scratch_shapes=[pltpu.VMEM((16, 256, 128), F32)],
@@ -268,7 +264,7 @@
         in_specs=[vmem] * count,
         out_specs=vmem,
         name="final_step",
-    )(*streams)
+    )(*[pltpu.with_memory_space_constraint(s, pltpu.VMEM) for s in streams])
     return out.reshape(2048, 2, 128).transpose(1, 0, 2).reshape(2, 262144)
 
 

time: 108 us -> 95.3 us (0.88)
  waiting for transfers between devices: 30.1 us -> 18.3 us
  starting transfers between devices: 56.3 us -> 65 us
  other arithmetic: 8.68 us -> 2.4 us
  Pallas kernels: 11.7 us -> 8.88 us
    ppermute x36, waiting for transfers between devices: 30.1 us -> 17.5 us  [shards(): got = lax.ppermute(streams[i], AXES, pairs_of('xyz'[k], first))]
    ppermute x36, starting transfers between devices: 51.9 us -> 63.7 us  [shards(): got = lax.ppermute(streams[i], AXES, pairs_of('xyz'[k], first))]
    ppermute x6, starting transfers between devices: 4.42 us -> 1.32 us  [shards(): got = lax.ppermute(streams[i], AXES, pairs_of('c', True))]
    add x6, other arithmetic: 2.46 us -> 0.25 us  [shards(): streams[i] = streams[i] + coef[9:10] * got]
    add x18, other arithmetic: 3.48 us -> 1.41 us  [shards(): streams[i] = kept[i] + got]
    add x18, other arithmetic: 2.74 us -> 0.74 us  [shards(): coef[3 * k + 1:3 * k + 2] * mine + coef[3 * k + 2:3 * k + 3] * got]
    pallas_call x1, Pallas kernels: 5.15 us -> 3.68 us  [shards(): pl.pallas_call(final_kernel, out_shape=jax.ShapeDtypeStruct((4096, 128),...]
    pallas_call x1, Pallas kernels: 6.5 us -> 5.2 us  [shards(): pl.pallas_call(local_kernel, out_shape=[pltpu.VMEM((s, 128), F32) for s i...]
  transfers between devices with their start and end apart: 42 -> 42, of which waited for: 16 -> 14; matrix products, arithmetic and copies ran while one was open for 8% -> 2% of each run, Pallas kernels for 0% -> 0%
where the time goes in v1:
time: 95.3 us; the launch traced here: 95 us
  starting transfers between devices  65 us (68%)
  waiting for transfers between devices  18.3 us (19%)
  Pallas kernels  8.88 us (9%)
  other arithmetic  2.4 us (3%)
    ppermute x36, starting transfers between devices, shards(): got = lax.ppermute(streams[i], AXES, pairs_of('xyz'[k], first))  63.7 us
    ppermute x36, waiting for transfers between devices, shards(): got = lax.ppermute(streams[i], AXES, pairs_of('xyz'[k], first))  17.5 us
    pallas_call x1, Pallas kernels, shards(): pl.pallas_call(local_kernel, out_shape=[pltpu.VMEM((s, 128), F32) for s i...  5.2 us
    pallas_call x1, Pallas kernels, shards(): pl.pallas_call(final_kernel, out_shape=jax.ShapeDtypeStruct((4096, 128),...  3.68 us
  transfers between devices with their start and end apart: 42, of which 14 were waited for; matrix products, arithmetic and copies ran while one was open for 2% of the time, Pallas kernels for 0%

profile of v1, /device:TPU:0, one launch (start us, length us, event | category | flops | bytes accessed | tf_op | source)
XLA Modules:
  0.0 95.0 jit_solution(18423586040422263680)
XLA Ops:
  0.0 5.2 %local_step.1 = (f32[656,128]{1,0:T(8,128)S(1)}, f32[672,128]{1,0:T(8,128)S(1)}, f32[680,128]{1,0:T(8,128)S(1)}, f32[688,128]{1,0:T(8,128)S(1)}, f32[696,128]{1,...) custom-call(f32[4096,128]{1,0:T(8,128)} %bitcast.30, f32[25]{0:T(128)} %j_ref.1, f32[25]{0:T(128)} %f_ref.1), custom_call_target="tpu_custom_call" | custom-call | tf_op jit(solution)/shard_map/local_step/pallas_call | solution.py:235
  10.8 2.0 %collective-permute-start.15 = (f32[680,128]{1,0:T(8,128)S(1)}, f32[680,128]{1,0:T(8,128)S(1)}, u32[]{:S(2)}, u32[]{:S(2)}) collective-permute-start(f32[680,128]{1,0:T(8,128)S(1)} %multiply_add_fusion.15), channel_id=1, source_target_pairs={{0,32},{1,33},{2,34},{3,35},{4,36},{5,37},{6,38},{7,39},{8,40},{9,... | collective-permute-start | bytes 1044488 | tf_op jit(solution)/shard_map/ppermute | solution.py:254
  14.6 2.0 %collective-permute-start.36 = (f32[704,128]{1,0:T(8,128)S(1)}, f32[704,128]{1,0:T(8,128)S(1)}, u32[]{:S(2)}, u32[]{:S(2)}) collective-permute-start(f32[704,128]{1,0:T(8,128)S(1)} %multiply_add_fusion.3), channel_id=1, source_target_pairs={{0,32},{1,33},{2,34},{3,35},{4,36},{5,37},{6,38},{7,39},{8,40},{9,... | collective-permute-start | bytes 1081352 | tf_op jit(solution)/shard_map/ppermute | solution.py:254
  16.7 2.8 %collective-permute-start.2 = (f32[656,128]{1,0:T(8,128)S(1)}, f32[656,128]{1,0:T(8,128)S(1)}, u32[]{:S(2)}, u32[]{:S(2)}) collective-permute-start(f32[656,128]{1,0:T(8,128)S(1)} %multiply_add_fusion.22), channel_id=1, source_target_pairs={{0,9},{1,8},{2,11},{3,10},{4,13},{5,12},{6,15},{7,14},{8,1},{9,0},... | collective-permute-start | bytes 1007624 | tf_op jit(solution)/shard_map/ppermute | solution.py:254
  19.6 3.1 %collective-permute-start.9 = (f32[672,128]{1,0:T(8,128)S(1)}, f32[672,128]{1,0:T(8,128)S(1)}, u32[]{:S(2)}, u32[]{:S(2)}) collective-permute-start(f32[672,128]{1,0:T(8,128)S(1)} %multiply_add_fusion.18), channel_id=1, source_target_pairs={{0,6},{1,7},{2,4},{3,5},{4,2},{5,3},{6,0},{7,1},{8,14},{9,15},{10,... | collective-permute-start | bytes 1032200 | tf_op jit(solution)/shard_map/ppermute | solution.py:254
  22.7 3.1 %collective-permute-start.16 = (f32[680,128]{1,0:T(8,128)S(1)}, f32[680,128]{1,0:T(8,128)S(1)}, u32[]{:S(2)}, u32[]{:S(2)}) collective-permute-start(f32[680,128]{1,0:T(8,128)S(1)} %multiply_add_fusion.14), channel_id=1, source_target_pairs={{0,96},{1,97},{2,98},{3,99},{4,100},{5,101},{6,102},{7,103},{8,104... | collective-permute-start | bytes 1044488 | tf_op jit(solution)/shard_map/ppermute | solution.py:254
  34.6 3.3 %collective-permute-done.30 = f32[696,128]{1,0:T(8,128)S(1)} collective-permute-done((f32[696,128]{1,0:T(8,128)S(1)}, f32[696,128]{1,0:T(8,128)S(1)}, u32[]{:S(2)}, u32[]{:S(2)}) %collective-permute-start.30) | collective-permute-done | bytes 356384 | tf_op jit(solution)/shard_map/ppermute | solution.py:254
  38.4 2.7 %collective-permute-start.38 = (f32[704,128]{1,0:T(8,128)S(1)}, f32[704,128]{1,0:T(8,128)S(1)}, u32[]{:S(2)}, u32[]{:S(2)}) collective-permute-start(f32[704,128]{1,0:T(8,128)S(1)} %add_add_fusion.2), channel_id=1, source_target_pairs={{0,8},{1,9},{2,10},{3,11},{4,12},{5,13},{6,14},{7,15},{8,0},{9,1},... | collective-permute-start | bytes 1081352 | tf_op jit(solution)/shard_map/ppermute | solution.py:254
  42.9 2.5 %collective-permute-start.11 = (f32[672,128]{1,0:T(8,128)S(1)}, f32[672,128]{1,0:T(8,128)S(1)}, u32[]{:S(2)}, u32[]{:S(2)}) collective-permute-start(f32[672,128]{1,0:T(8,128)S(1)} %multiply_add_fusion.17), channel_id=1, source_target_pairs={{0,96},{1,97},{2,98},{3,99},{4,100},{5,101},{6,102},{7,103},{8,104... | collective-permute-start | bytes 1032200 | tf_op jit(solution)/shard_map/ppermute | solution.py:254
  46.2 3.1 %collective-permute-start.18 = (f32[680,128]{1,0:T(8,128)S(1)}, f32[680,128]{1,0:T(8,128)S(1)}, u32[]{:S(2)}, u32[]{:S(2)}) collective-permute-start(f32[680,128]{1,0:T(8,128)S(1)} %multiply_add_fusion.13), channel_id=1, source_target_pairs={{0,9},{1,8},{2,11},{3,10},{4,13},{5,12},{6,15},{7,14},{8,1},{9,0},... | collective-permute-start | bytes 1044488 | tf_op jit(solution)/shard_map/ppermute | solution.py:254
  49.4 2.4 %collective-permute-start.25 = (f32[688,128]{1,0:T(8,128)S(1)}, f32[688,128]{1,0:T(8,128)S(1)}, u32[]{:S(2)}, u32[]{:S(2)}) collective-permute-start(f32[688,128]{1,0:T(8,128)S(1)} %multiply_add_fusion.9), channel_id=1, source_target_pairs={{0,6},{1,7},{2,4},{3,5},{4,2},{5,3},{6,0},{7,1},{8,14},{9,15},{10,... | collective-permute-start | bytes 1056776 | tf_op jit(solution)/shard_map/ppermute | solution.py:254
  51.9 3.2 %collective-permute-start.32 = (f32[696,128]{1,0:T(8,128)S(1)}, f32[696,128]{1,0:T(8,128)S(1)}, u32[]{:S(2)}, u32[]{:S(2)}) collective-permute-start(f32[696,128]{1,0:T(8,128)S(1)} %multiply_add_fusion.5), channel_id=1, source_target_pairs={{0,96},{1,97},{2,98},{3,99},{4,100},{5,101},{6,102},{7,103},{8,104... | collective-permute-start | bytes 1069064 | tf_op jit(solution)/shard_map/ppermute | solution.py:254
  55.1 1.7 %collective-permute-start.39 = (f32[704,128]{1,0:T(8,128)S(1)}, f32[704,128]{1,0:T(8,128)S(1)}, u32[]{:S(2)}, u32[]{:S(2)}) collective-permute-start(f32[704,128]{1,0:T(8,128)S(1)} %multiply_add_fusion.1), channel_id=1, source_target_pairs={{0,9},{1,8},{2,11},{3,10},{4,13},{5,12},{6,15},{7,14},{8,1},{9,0},... | collective-permute-start | bytes 1081352 | tf_op jit(solution)/shard_map/ppermute | solution.py:254
  58.0 2.0 %collective-permute-start.12 = (f32[672,128]{1,0:T(8,128)S(1)}, f32[672,128]{1,0:T(8,128)S(1)}, u32[]{:S(2)}, u32[]{:S(2)}) collective-permute-start(f32[672,128]{1,0:T(8,128)S(1)} %add_add_fusion.13), channel_id=1, source_target_pairs={{0,8},{1,9},{2,10},{3,11},{4,12},{5,13},{6,14},{7,15},{8,0},{9,1},... | collective-permute-start | bytes 1032200 | tf_op jit(solution)/shard_map/ppermute | solution.py:254
  60.2 3.1 %collective-permute-done.32 = f32[696,128]{1,0:T(8,128)S(1)} collective-permute-done((f32[696,128]{1,0:T(8,128)S(1)}, f32[696,128]{1,0:T(8,128)S(1)}, u32[]{:S(2)}, u32[]{:S(2)}) %collective-permute-start.32) | collective-permute-done | bytes 356384 | tf_op jit(solution)/shard_map/ppermute | solution.py:254
  66.1 2.9 %collective-permute-start.33 = (f32[696,128]{1,0:T(8,128)S(1)}, f32[696,128]{1,0:T(8,128)S(1)}, u32[]{:S(2)}, u32[]{:S(2)}) collective-permute-start(f32[696,128]{1,0:T(8,128)S(1)} %add_add_fusion.4), channel_id=1, source_target_pairs={{0,8},{1,9},{2,10},{3,11},{4,12},{5,13},{6,14},{7,15},{8,0},{9,1},... | collective-permute-start | bytes 1069064 | tf_op jit(solution)/shard_map/ppermute | solution.py:254
  70.7 2.6 %collective-permute-start.13 = (f32[672,128]{1,0:T(8,128)S(1)}, f32[672,128]{1,0:T(8,128)S(1)}, u32[]{:S(2)}, u32[]{:S(2)}) collective-permute-start(f32[672,128]{1,0:T(8,128)S(1)} %multiply_add_fusion.16), channel_id=1, source_target_pairs={{0,9},{1,8},{2,11},{3,10},{4,13},{5,12},{6,15},{7,14},{8,1},{9,0},... | collective-permute-start | bytes 1032200 | tf_op jit(solution)/shard_map/ppermute | solution.py:254
  73.9 3.4 %collective-permute-start.20 = (f32[680,128]{1,0:T(8,128)S(1)}, f32[680,128]{1,0:T(8,128)S(1)}, u32[]{:S(2)}, u32[]{:S(2)}) collective-permute-start(f32[680,128]{1,0:T(8,128)S(1)} %multiply_add_fusion.12), channel_id=1, source_target_pairs={{0,6},{1,7},{2,4},{3,5},{4,2},{5,3},{6,0},{7,1},{8,14},{9,15},{10,... | collective-permute-start | bytes 1044488 | tf_op jit(solution)/shard_map/ppermute | solution.py:254
  77.6 1.9 %collective-permute-start.27 = (f32[688,128]{1,0:T(8,128)S(1)}, f32[688,128]{1,0:T(8,128)S(1)}, u32[]{:S(2)}, u32[]{:S(2)}) collective-permute-start(f32[688,128]{1,0:T(8,128)S(1)} %multiply_add_fusion.8), channel_id=1, source_target_pairs={{0,96},{1,97},{2,98},{3,99},{4,100},{5,101},{6,102},{7,103},{8,104... | collective-permute-start | bytes 1056776 | tf_op jit(solution)/shard_map/ppermute | solution.py:254
  79.5 2.3 %collective-permute-start.34 = (f32[696,128]{1,0:T(8,128)S(1)}, f32[696,128]{1,0:T(8,128)S(1)}, u32[]{:S(2)}, u32[]{:S(2)}) collective-permute-start(f32[696,128]{1,0:T(8,128)S(1)} %multiply_add_fusion.4), channel_id=1, source_target_pairs={{0,9},{1,8},{2,11},{3,10},{4,13},{5,12},{6,15},{7,14},{8,1},{9,0},... | collective-permute-start | bytes 1069064 | tf_op jit(solution)/shard_map/ppermute | solution.py:254
  81.9 4.0 %collective-permute-start.41 = (f32[704,128]{1,0:T(8,128)S(1)}, f32[704,128]{1,0:T(8,128)S(1)}, u32[]{:S(2)}, u32[]{:S(2)}) collective-permute-start(f32[704,128]{1,0:T(8,128)S(1)} %multiply_add_fusion), channel_id=1, source_target_pairs={{0,6},{1,7},{2,4},{3,5},{4,2},{5,3},{6,0},{7,1},{8,14},{9,15},{10,... | collective-permute-start | bytes 1081352 | tf_op jit(solution)/shard_map/ppermute | solution.py:254
  86.2 2.0 %collective-permute-done.34 = f32[696,128]{1,0:T(8,128)S(1)} collective-permute-done((f32[696,128]{1,0:T(8,128)S(1)}, f32[696,128]{1,0:T(8,128)S(1)}, u32[]{:S(2)}, u32[]{:S(2)}) %collective-permute-start.34) | collective-permute-done | bytes 356384 | tf_op jit(solution)/shard_map/ppermute | solution.py:254
  88.3 3.0 %collective-permute-done.41 = f32[704,128]{1,0:T(8,128)S(1)} collective-permute-done((f32[704,128]{1,0:T(8,128)S(1)}, f32[704,128]{1,0:T(8,128)S(1)}, u32[]{:S(2)}, u32[]{:S(2)}) %collective-permute-start.41) | collective-permute-done | bytes 360480 | tf_op jit(solution)/shard_map/ppermute | solution.py:254
  91.3 3.7 %final_step.1 = f32[4096,128]{1,0:T(8,128)} custom-call(f32[656,128]{1,0:T(8,128)S(1)} %add_add_fusion.15.refs_0_, f32[672,128]{1,0:T(8,128)S(1)} %add_add_fusion.12.refs_1_, f32[680,128]{1,0:T(8,128)S(1)} %add_add_fusion.9.refs_2_, f32[688,128]{1,0:T(8,128)S(1)} %add_add_fusion.6.refs_3_, f32[696,128]{1,0:T(8,128)S(1)} %add_add_fusion.3.refs_4_, ...), custom_call_target="tpu_custom_call" | custom-call | tf_op jit(solution)/shard_map/final_step/pallas_call | solution.py:261
  (105 shorter events, 26.6 us)
Async XLA Ops:
  12.8 9.9 %collective-permute-start.22 = (f32[688,128]{1,0:T(8,128)S(1)}, f32[688,128]{1,0:T(8,128)S(1)}, u32[]{:S(2)}, u32[]{:S(2)}) collective-permute-start(f32[688,128]{1,0:T(8,128)S(1)} %multiply_add_fusion.11), channel_id=1, source_target_pairs={{0,8},{1,9},{2,10},{3,11},{4,12},{5,13},{6,14},{7,15},{8,0},{9,1},... | collective-permute-start | bytes 1056776 | tf_op jit(solution)/shard_map/ppermute | solution.py:254
  13.5 12.4 %collective-permute-start.29 = (f32[696,128]{1,0:T(8,128)S(1)}, f32[696,128]{1,0:T(8,128)S(1)}, u32[]{:S(2)}, u32[]{:S(2)}) collective-permute-start(f32[696,128]{1,0:T(8,128)S(1)} %multiply_add_fusion.7), channel_id=1, source_target_pairs={{0,2},{1,3},{2,0},{3,1},{4,6},{5,7},{6,4},{7,5},{8,10},{9,11},{10,... | collective-permute-start | bytes 1069064 | tf_op jit(solution)/shard_map/ppermute | solution.py:254
  14.6 12.6 %collective-permute-start.36 = (f32[704,128]{1,0:T(8,128)S(1)}, f32[704,128]{1,0:T(8,128)S(1)}, u32[]{:S(2)}, u32[]{:S(2)}) collective-permute-start(f32[704,128]{1,0:T(8,128)S(1)} %multiply_add_fusion.3), channel_id=1, source_target_pairs={{0,32},{1,33},{2,34},{3,35},{4,36},{5,37},{6,38},{7,39},{8,40},{9,... | collective-permute-start | bytes 1081352 | tf_op jit(solution)/shard_map/ppermute | solution.py:254
  16.7 11.9 %collective-permute-start.2 = (f32[656,128]{1,0:T(8,128)S(1)}, f32[656,128]{1,0:T(8,128)S(1)}, u32[]{:S(2)}, u32[]{:S(2)}) collective-permute-start(f32[656,128]{1,0:T(8,128)S(1)} %multiply_add_fusion.22), channel_id=1, source_target_pairs={{0,9},{1,8},{2,11},{3,10},{4,13},{5,12},{6,15},{7,14},{8,1},{9,0},... | collective-permute-start | bytes 1007624 | tf_op jit(solution)/shard_map/ppermute | solution.py:254
  19.6 10.7 %collective-permute-start.9 = (f32[672,128]{1,0:T(8,128)S(1)}, f32[672,128]{1,0:T(8,128)S(1)}, u32[]{:S(2)}, u32[]{:S(2)}) collective-permute-start(f32[672,128]{1,0:T(8,128)S(1)} %multiply_add_fusion.18), channel_id=1, source_target_pairs={{0,6},{1,7},{2,4},{3,5},{4,2},{5,3},{6,0},{7,1},{8,14},{9,15},{10,... | collective-permute-start | bytes 1032200 | tf_op jit(solution)/shard_map/ppermute | solution.py:254
  27.2 10.7 %collective-permute-start.30 = (f32[696,128]{1,0:T(8,128)S(1)}, f32[696,128]{1,0:T(8,128)S(1)}, u32[]{:S(2)}, u32[]{:S(2)}) collective-permute-start(f32[696,128]{1,0:T(8,128)S(1)} %multiply_add_fusion.6), channel_id=1, source_target_pairs={{0,6},{1,7},{2,4},{3,5},{4,2},{5,3},{6,0},{7,1},{8,14},{9,15},{10,... | collective-permute-start | bytes 1069064 | tf_op jit(solution)/shard_map/ppermute | solution.py:254
  31.3 10.4 %collective-permute-start.10 = (f32[672,128]{1,0:T(8,128)S(1)}, f32[672,128]{1,0:T(8,128)S(1)}, u32[]{:S(2)}, u32[]{:S(2)}) collective-permute-start(f32[672,128]{1,0:T(8,128)S(1)} %add_add_fusion.14), channel_id=1, source_target_pairs={{0,32},{1,33},{2,34},{3,35},{4,36},{5,37},{6,38},{7,39},{8,40},{9,... | collective-permute-start | bytes 1032200 | tf_op jit(solution)/shard_map/ppermute | solution.py:254
  38.0 11.4 %collective-permute-start.31 = (f32[696,128]{1,0:T(8,128)S(1)}, f32[696,128]{1,0:T(8,128)S(1)}, u32[]{:S(2)}, u32[]{:S(2)}) collective-permute-start(f32[696,128]{1,0:T(8,128)S(1)} %add_add_fusion.5), channel_id=1, source_target_pairs={{0,32},{1,33},{2,34},{3,35},{4,36},{5,37},{6,38},{7,39},{8,40},{9,... | collective-permute-start | bytes 1069064 | tf_op jit(solution)/shard_map/ppermute | solution.py:254
  38.4 13.5 %collective-permute-start.38 = (f32[704,128]{1,0:T(8,128)S(1)}, f32[704,128]{1,0:T(8,128)S(1)}, u32[]{:S(2)}, u32[]{:S(2)}) collective-permute-start(f32[704,128]{1,0:T(8,128)S(1)} %add_add_fusion.2), channel_id=1, source_target_pairs={{0,8},{1,9},{2,10},{3,11},{4,12},{5,13},{6,14},{7,15},{8,0},{9,1},... | collective-permute-start | bytes 1081352 | tf_op jit(solution)/shard_map/ppermute | solution.py:254
  41.7 13.4 %collective-permute-start.4 = (f32[656,128]{1,0:T(8,128)S(1)}, f32[656,128]{1,0:T(8,128)S(1)}, u32[]{:S(2)}, u32[]{:S(2)}) collective-permute-start(f32[656,128]{1,0:T(8,128)S(1)} %multiply_add_fusion.21), channel_id=1, source_target_pairs={{0,6},{1,7},{2,4},{3,5},{4,2},{5,3},{6,0},{7,1},{8,14},{9,15},{10,... | collective-permute-start | bytes 1007624 | tf_op jit(solution)/shard_map/ppermute | solution.py:254
  42.9 14.0 %collective-permute-start.11 = (f32[672,128]{1,0:T(8,128)S(1)}, f32[672,128]{1,0:T(8,128)S(1)}, u32[]{:S(2)}, u32[]{:S(2)}) collective-permute-start(f32[672,128]{1,0:T(8,128)S(1)} %multiply_add_fusion.17), channel_id=1, source_target_pairs={{0,96},{1,97},{2,98},{3,99},{4,100},{5,101},{6,102},{7,103},{8,104... | collective-permute-start | bytes 1032200 | tf_op jit(solution)/shard_map/ppermute | solution.py:254
  46.2 11.8 %collective-permute-start.18 = (f32[680,128]{1,0:T(8,128)S(1)}, f32[680,128]{1,0:T(8,128)S(1)}, u32[]{:S(2)}, u32[]{:S(2)}) collective-permute-start(f32[680,128]{1,0:T(8,128)S(1)} %multiply_add_fusion.13), channel_id=1, source_target_pairs={{0,9},{1,8},{2,11},{3,10},{4,13},{5,12},{6,15},{7,14},{8,1},{9,0},... | collective-permute-start | bytes 1044488 | tf_op jit(solution)/shard_map/ppermute | solution.py:254
  49.4 10.6 %collective-permute-start.25 = (f32[688,128]{1,0:T(8,128)S(1)}, f32[688,128]{1,0:T(8,128)S(1)}, u32[]{:S(2)}, u32[]{:S(2)}) collective-permute-start(f32[688,128]{1,0:T(8,128)S(1)} %multiply_add_fusion.9), channel_id=1, source_target_pairs={{0,6},{1,7},{2,4},{3,5},{4,2},{5,3},{6,0},{7,1},{8,14},{9,15},{10,... | collective-permute-start | bytes 1056776 | tf_op jit(solution)/shard_map/ppermute | solution.py:254
  51.9 11.4 %collective-permute-start.32 = (f32[696,128]{1,0:T(8,128)S(1)}, f32[696,128]{1,0:T(8,128)S(1)}, u32[]{:S(2)}, u32[]{:S(2)}) collective-permute-start(f32[696,128]{1,0:T(8,128)S(1)} %multiply_add_fusion.5), channel_id=1, source_target_pairs={{0,96},{1,97},{2,98},{3,99},{4,100},{5,101},{6,102},{7,103},{8,104... | collective-permute-start | bytes 1069064 | tf_op jit(solution)/shard_map/ppermute | solution.py:254
  55.1 11.0 %collective-permute-start.39 = (f32[704,128]{1,0:T(8,128)S(1)}, f32[704,128]{1,0:T(8,128)S(1)}, u32[]{:S(2)}, u32[]{:S(2)}) collective-permute-start(f32[704,128]{1,0:T(8,128)S(1)} %multiply_add_fusion.1), channel_id=1, source_target_pairs={{0,9},{1,8},{2,11},{3,10},{4,13},{5,12},{6,15},{7,14},{8,1},{9,0},... | collective-permute-start | bytes 1081352 | tf_op jit(solution)/shard_map/ppermute | solution.py:254
  57.0 12.1 %collective-permute-start.5 = (f32[656,128]{1,0:T(8,128)S(1)}, f32[656,128]{1,0:T(8,128)S(1)}, u32[]{:S(2)}, u32[]{:S(2)}) collective-permute-start(f32[656,128]{1,0:T(8,128)S(1)} %add_add_fusion.16), channel_id=1, source_target_pairs={{0,32},{1,33},{2,34},{3,35},{4,36},{5,37},{6,38},{7,39},{8,40},{9,... | collective-permute-start | bytes 1007624 | tf_op jit(solution)/shard_map/ppermute | solution.py:254
  58.0 11.3 %collective-permute-start.12 = (f32[672,128]{1,0:T(8,128)S(1)}, f32[672,128]{1,0:T(8,128)S(1)}, u32[]{:S(2)}, u32[]{:S(2)}) collective-permute-start(f32[672,128]{1,0:T(8,128)S(1)} %add_add_fusion.13), channel_id=1, source_target_pairs={{0,8},{1,9},{2,10},{3,11},{4,12},{5,13},{6,14},{7,15},{8,0},{9,1},... | collective-permute-start | bytes 1032200 | tf_op jit(solution)/shard_map/ppermute | solution.py:254
  60.0 10.6 %collective-permute-start.19 = (f32[680,128]{1,0:T(8,128)S(1)}, f32[680,128]{1,0:T(8,128)S(1)}, u32[]{:S(2)}, u32[]{:S(2)}) collective-permute-start(f32[680,128]{1,0:T(8,128)S(1)} %add_add_fusion.10), channel_id=1, source_target_pairs={{0,2},{1,3},{2,0},{3,1},{4,6},{5,7},{6,4},{7,5},{8,10},{9,11},{10,... | collective-permute-start | bytes 1044488 | tf_op jit(solution)/shard_map/ppermute | solution.py:254
  63.3 10.6 %collective-permute-start.26 = (f32[688,128]{1,0:T(8,128)S(1)}, f32[688,128]{1,0:T(8,128)S(1)}, u32[]{:S(2)}, u32[]{:S(2)}) collective-permute-start(f32[688,128]{1,0:T(8,128)S(1)} %add_add_fusion.7), channel_id=1, source_target_pairs={{0,32},{1,33},{2,34},{3,35},{4,36},{5,37},{6,38},{7,39},{8,40},{9,... | collective-permute-start | bytes 1056776 | tf_op jit(solution)/shard_map/ppermute | solution.py:254
  66.1 11.5 %collective-permute-start.33 = (f32[696,128]{1,0:T(8,128)S(1)}, f32[696,128]{1,0:T(8,128)S(1)}, u32[]{:S(2)}, u32[]{:S(2)}) collective-permute-start(f32[696,128]{1,0:T(8,128)S(1)} %add_add_fusion.4), channel_id=1, source_target_pairs={{0,8},{1,9},{2,10},{3,11},{4,12},{5,13},{6,14},{7,15},{8,0},{9,1},... | collective-permute-start | bytes 1069064 | tf_op jit(solution)/shard_map/ppermute | solution.py:254
  69.1 10.4 %collective-permute-start.40 = (f32[704,128]{1,0:T(8,128)S(1)}, f32[704,128]{1,0:T(8,128)S(1)}, u32[]{:S(2)}, u32[]{:S(2)}) collective-permute-start(f32[704,128]{1,0:T(8,128)S(1)} %add_add_fusion.1), channel_id=1, source_target_pairs={{0,2},{1,3},{2,0},{3,1},{4,6},{5,7},{6,4},{7,5},{8,10},{9,11},{10,... | collective-permute-start | bytes 1081352 | tf_op jit(solution)/shard_map/ppermute | solution.py:254
  69.3 12.6 %collective-permute-start.6 = (f32[656,128]{1,0:T(8,128)S(1)}, f32[656,128]{1,0:T(8,128)S(1)}, u32[]{:S(2)}, u32[]{:S(2)}) collective-permute-start(f32[656,128]{1,0:T(8,128)S(1)} %multiply_add_fusion.20), channel_id=1, source_target_pairs={{0,96},{1,97},{2,98},{3,99},{4,100},{5,101},{6,102},{7,103},{8,104... | collective-permute-start | bytes 1007624 | tf_op jit(solution)/shard_map/ppermute | solution.py:254
  70.7 15.3 %collective-permute-start.13 = (f32[672,128]{1,0:T(8,128)S(1)}, f32[672,128]{1,0:T(8,128)S(1)}, u32[]{:S(2)}, u32[]{:S(2)}) collective-permute-start(f32[672,128]{1,0:T(8,128)S(1)} %multiply_add_fusion.16), channel_id=1, source_target_pairs={{0,9},{1,8},{2,11},{3,10},{4,13},{5,12},{6,15},{7,14},{8,1},{9,0},... | collective-permute-start | bytes 1032200 | tf_op jit(solution)/shard_map/ppermute | solution.py:254
  73.9 12.1 %collective-permute-start.20 = (f32[680,128]{1,0:T(8,128)S(1)}, f32[680,128]{1,0:T(8,128)S(1)}, u32[]{:S(2)}, u32[]{:S(2)}) collective-permute-start(f32[680,128]{1,0:T(8,128)S(1)} %multiply_add_fusion.12), channel_id=1, source_target_pairs={{0,6},{1,7},{2,4},{3,5},{4,2},{5,3},{6,0},{7,1},{8,14},{9,15},{10,... | collective-permute-start | bytes 1044488 | tf_op jit(solution)/shard_map/ppermute | solution.py:254
  (18 other events, 126.7 us)

commit v2 on v1

--- a/solution.py
+++ b/solution.py
@@ -7,8 +7,12 @@
 
 
 AXES = ("gx", "gy", "gz")
-SIZES = (656, 672, 680, 688, 696, 704)
-STARTS = tuple(sum(SIZES[:i]) for i in range(len(SIZES)))
+SHAPES = ((688, 128), (680, 128), (85, 8, 128), (43, 16, 128), (5, 136, 128), (17, 40, 128))
+ROWS = (688, 680, 680, 688, 680, 680)
+FIRST_DIM = (0, 1, 2, 0, 1, 2)
+COUNT = len(SHAPES)
+HALF = COUNT // 2
+BASES = tuple(sum(ROWS[:i]) for i in range(COUNT))
 F32 = jnp.float32
 BF16 = jnp.bfloat16
 
@@ -83,8 +87,23 @@
     return number
 
 
-def local_kernel(x_ref, j_ref, f_ref, *refs):
-    outs, coef_ref, z_ref = refs[: len(SIZES)], refs[len(SIZES)], refs[len(SIZES) + 1]
+def window(refs, base, row, rows):
+    s = max(i for i in range(base, base + len(refs)) if BASES[i] <= row)
+    at = row - BASES[s]
+    if len(SHAPES[s]) == 2:
+        return refs[s - base], (slice(at, at + rows), slice(None))
+    per = SHAPES[s][1]
+    return refs[s - base], (at // per, slice(at % per, at % per + rows), slice(None))
+
+
+def phase_kernel(x_hbm, j_ref, f_ref, *refs):
+    outs, (coef_ref, lane_ref, high_ref, x_ref, sems) = refs[:COUNT], refs[COUNT:]
+    copies = [
+        pltpu.make_async_copy(x_hbm.at[pl.ds(1024 * h, 1024), :], x_ref.at[pl.ds(1024 * h, 1024), :], sems.at[h])
+        for h in range(4)
+    ]
+    for copy in copies:
+        copy.start()
     number = device_bits()
     bits = [(number >> k) & 1 for k in range(7)]
     sigma = [1.0 - 2.0 * b.astype(F32) for b in bits]
@@ -134,123 +153,129 @@
     device_ones = bits[0] + bits[1] + bits[2] + bits[3] + bits[4] + bits[5] + bits[6]
     e2r, e2i = turn(jnp.cos(phase), jnp.sin(phase), ones_in(high, 7) + device_ones)
     e2r, e2i = e2r * scale, e2i * scale
+    columns = [
+        [jnp.transpose(jnp.broadcast_to(e[v : v + 1, :], (128, 128))) for e in (e2r, e2i)] for v in range(2)
+    ]
 
     lane_hi, lane_lo = split(rotation(tangents, 0, True))
-    lane_mat = jnp.concatenate(
-        [
-            jnp.concatenate([lane_hi, lane_lo], axis=1),
-            jnp.concatenate([lane_hi, jnp.zeros((128, 128), BF16)], axis=1),
-        ],
-        axis=0,
-    )
-    row_rot = rotation(tangents, 11, False)
-    row_mats = []
-    for v in range(2):
-        mr, mi = row_rot * e2r[v : v + 1, :], row_rot * e2i[v : v + 1, :]
-        row_mats.append(
-            split(
-                jnp.concatenate(
-                    [jnp.concatenate([mr, -mi], axis=1), jnp.concatenate([mi, mr], axis=1)], axis=0
-                )
-            )
-        )
-
-    def lanes_done(rl):
-        xre = x_ref[pl.ds(2 * rl, 128, stride=32), :]
-        xim = x_ref[pl.ds(2 * rl + 1, 128, stride=32), :]
-        er, ei = e1r[rl : rl + 1, :], e1i[rl : rl + 1, :]
-        y = jnp.concatenate([xre * er - xim * ei, xre * ei + xim * er], axis=0)
-        y_hi, y_lo = split(y)
-        p = jnp.dot(jnp.concatenate([y_hi, y_lo], axis=1), lane_mat, preferred_element_type=F32)
-        return p[:, :128] + p[:, 128:]
-
-    for rl in range(0, 16, 2):
-        m_hi, m_lo = row_mats[rl >> 3]
-        y_hi, y_lo = split(jnp.concatenate([lanes_done(rl), lanes_done(rl + 1)], axis=1))
-        z = jnp.dot(m_hi, y_hi, preferred_element_type=F32)
-        z = z + jnp.dot(m_lo, y_hi, preferred_element_type=F32)
-        z = z + jnp.dot(m_hi, y_lo, preferred_element_type=F32)
-        z_ref[rl] = z[:, :128]
-        z_ref[rl + 1] = z[:, 128:]
+    lane_ref[0:128, 0:128] = lane_hi
+    lane_ref[0:128, 128:256] = lane_lo
+    lane_ref[128:256, 0:128] = lane_hi
+    lane_ref[128:256, 128:256] = jnp.zeros((128, 128), BF16)
+    high_hi, high_lo = split(rotation(tangents, 11, False))
+    high_ref[:, 0:128] = high_hi
+    high_ref[:, 128:256] = high_lo
+    high_ref[:, 256:384] = high_hi
 
     low_tangents = [jnp.broadcast_to(tangents[7 + k : 8 + k, :], (8, 128)) for k in range(4)]
-    for at in range(0, 256, 8):
-        v = [z_ref[rl, at : at + 8, :] for rl in range(16)]
-        for k in range(4):
-            t = low_tangents[k]
-            w = list(v)
+    for at in range(0, 128, 8):
+        if at % 32 == 0:
+            copies[at // 32].wait()
+        values = [[], []]
+        for rl in range(16):
+            xre = x_ref[pl.ds(at * 32 + 2 * rl, 8, stride=32), :]
+            xim = x_ref[pl.ds(at * 32 + 2 * rl + 1, 8, stride=32), :]
+            er, ei = e1r[rl : rl + 1, :], e1i[rl : rl + 1, :]
+            cr, ci = (c[at : at + 8, :] for c in columns[rl >> 3])
+            yre, yim = xre * er - xim * ei, xre * ei + xim * er
+            values[0].append(yre * cr - yim * ci)
+            values[1].append(yre * ci + yim * cr)
+        for c in range(2):
+            v = values[c]
+            for k in range(4):
+                t = low_tangents[k]
+                v = [
+                    v[rl] + t * v[rl ^ (1 << k)] if rl >> k & 1 else v[rl] - t * v[rl ^ (1 << k)]
+                    for rl in range(16)
+                ]
             for rl in range(16):
-                if rl >> k & 1:
-                    w[rl] = v[rl] + t * v[rl ^ (1 << k)]
-                else:
-                    w[rl] = v[rl] - t * v[rl ^ (1 << k)]
-            v = w
-        for rl in range(16):
-            row = rl * 256 + at
-            s = max(i for i in range(len(SIZES)) if STARTS[i] <= row)
-            outs[s][row - STARTS[s] : row - STARTS[s] + 8, :] = v[rl]
-
-
-def final_kernel(*refs):
-    ins, out_ref = refs[: len(SIZES)], refs[len(SIZES)]
+                ref, index = window(outs, 0, (2 * rl + c) * 128 + at, 8)
+                ref[index] = v[rl]
+
+
+def finish(ins, base, lane_ref, high_ref, out_hbm, o_ref, sems):
     number = device_bits()
     device_ones = number & 1
     for k in range(1, 7):
         device_ones = device_ones + ((number >> k) & 1)
     rows = lax.broadcasted_iota(jnp.int32, (128, 128), 0)
     cols = lax.broadcasted_iota(jnp.int32, (128, 128), 1)
-    base = ones_in(rows, 7) + ones_in(cols, 7) + device_ones
-
-    def read(start):
+    turns = ones_in(rows, 7) + ones_in(cols, 7) + device_ones
+    first = 0 if base == 0 else 8
+
+    def read(row):
         parts = []
-        row = start
-        while row < start + 128:
-            s = max(i for i in range(len(SIZES)) if STARTS[i] <= row)
-            stop = min(start + 128, STARTS[s] + SIZES[s])
-            parts.append(ins[s][row - STARTS[s] : stop - STARTS[s], :])
-            row = stop
-        return parts[0] if len(parts) == 1 else jnp.concatenate(parts, axis=0)
-
-    for rl in range(16):
-        re, im = read(rl * 256), read(rl * 256 + 128)
-        quarter = (base + bin(rl).count("1")) & 3
+        for at in range(row, row + 128, 8):
+            ref, index = window(ins, base, at, 8)
+            parts.append(ref[index])
+        return jnp.concatenate(parts, axis=0)
+
+    copies = []
+    for rl in range(first, first + 8):
+        y = jnp.concatenate([read(rl * 256), read(rl * 256 + 128)], axis=0)
+        y_hi, y_lo = split(y)
+        p = jnp.dot(jnp.concatenate([y_hi, y_lo], axis=1), lane_ref[...], preferred_element_type=F32)
+        y = p[:, :128] + p[:, 128:]
+        y_hi, y_lo = split(jnp.concatenate([y[:128], y[128:]], axis=1))
+        z = jnp.dot(high_ref[...], jnp.concatenate([y_hi, y_hi, y_lo], axis=0), preferred_element_type=F32)
+        re, im = z[:, :128], z[:, 128:]
+        quarter = (turns + bin(rl).count("1")) & 3
         odd = (quarter & 1) == 1
         out_re = jnp.where(odd, im, re)
         out_im = jnp.where(odd, re, im)
-        out_ref[pl.ds(2 * rl, 128, stride=32), :] = jnp.where(quarter >= 2, -out_re, out_re)
-        out_ref[pl.ds(2 * rl + 1, 128, stride=32), :] = jnp.where(
-            (quarter == 1) | (quarter == 2), -out_im, out_im
-        )
+        at = 2 * (rl - first)
+        o_ref[pl.ds(at, 128, stride=16), :] = jnp.where(quarter >= 2, -out_re, out_re)
+        o_ref[pl.ds(at + 1, 128, stride=16), :] = jnp.where((quarter == 1) | (quarter == 2), -out_im, out_im)
+        if rl % 4 == 3:
+            part = (rl - first) // 4
+            copies.append(
+                pltpu.make_async_copy(
+                    o_ref.reshape(128, 16, 128).at[:, pl.ds(8 * part, 8), :],
+                    out_hbm.at[:, pl.ds(2 * first + 8 * part, 8), :],
+                    sems.at[part],
+                )
+            )
+            copies[-1].start()
+    for copy in copies:
+        copy.wait()
+
+
+def first_final_kernel(*refs):
+    finish(refs[:HALF], 0, *refs[HALF:])
+
+
+def second_final_kernel(*refs):
+    finish(refs[:HALF], HALF, refs[HALF], refs[HALF + 1], *refs[HALF + 3 :])
 
 
 def exchange_order():
-    count = len(SIZES)
-    return [(i, step) for step in ("c", 0, 1, 2, 3, 4, 5) for i in range(count)]
+    return [(i, step) for step in ("c", 0, 1, 2, 3, 4, 5) for i in range(COUNT)]
 
 
 def shards(amplitudes, couplings, fields):
     rows = amplitudes.reshape(2, 2048, 128).transpose(1, 0, 2).reshape(4096, 128)
     vmem = pl.BlockSpec(memory_space=pltpu.VMEM)
     smem = pl.BlockSpec(memory_space=pltpu.SMEM)
+    hbm = pl.BlockSpec(memory_space=pl.ANY)
     made = pl.pallas_call(
-        local_kernel,
-        out_shape=[pltpu.VMEM((s, 128), F32) for s in SIZES] + [pltpu.VMEM((16, 128), F32)],
-        in_specs=[vmem, smem, smem],
-        out_specs=[vmem] * (len(SIZES) + 1),
-        scratch_shapes=[pltpu.VMEM((16, 256, 128), F32)],
-        name="local_step",
+        phase_kernel,
+        out_shape=[pltpu.VMEM(s, F32) for s in SHAPES]
+        + [pltpu.VMEM((16, 128), F32), pltpu.VMEM((256, 256), BF16), pltpu.VMEM((128, 384), BF16)],
+        in_specs=[hbm, smem, smem],
+        out_specs=[vmem] * (COUNT + 3),
+        scratch_shapes=[pltpu.VMEM((4096, 128), F32), pltpu.SemaphoreType.DMA((4,))],
+        name="phase_step",
     )(rows, couplings, fields)
-    streams, coef = list(made[:-1]), made[-1]
-
-    count = len(streams)
-    kept = [None] * count
+    streams, (coef, lane_mat, high_mat) = list(made[:COUNT]), made[COUNT:]
+
+    kept = [None] * COUNT
     for i, step in exchange_order():
         if step == "c":
             got = lax.ppermute(streams[i], AXES, pairs_of("c", True))
             streams[i] = streams[i] + coef[9:10] * got
             continue
         first = step % 2 == 0
-        k = (step // 2 + i) % 3
+        k = (step // 2 + FIRST_DIM[i]) % 3
         got = lax.ppermute(streams[i], AXES, pairs_of("xyz"[k], first))
         if first:
             mine = streams[i]
@@ -258,13 +283,31 @@
             streams[i] = coef[3 * k + 1 : 3 * k + 2] * mine + coef[3 * k + 2 : 3 * k + 3] * got
         else:
             streams[i] = kept[i] + got
+
+    def held(value):
+        return pltpu.with_memory_space_constraint(value, pltpu.VMEM)
+
+    scratch = [pltpu.VMEM((2048, 128), F32), pltpu.SemaphoreType.DMA((2,))]
+    out_shape = jax.ShapeDtypeStruct((128, 32, 128), F32)
     out = pl.pallas_call(
-        final_kernel,
-        out_shape=jax.ShapeDtypeStruct((4096, 128), F32),
-        in_specs=[vmem] * count,
-        out_specs=vmem,
-        name="final_step",
-    )(*[pltpu.with_memory_space_constraint(s, pltpu.VMEM) for s in streams])
+        first_final_kernel,
+        out_shape=out_shape,
+        in_specs=[vmem] * (HALF + 2),
+        out_specs=hbm,
+        scratch_shapes=scratch,
+        compiler_params=pltpu.CompilerParams(vmem_limit_bytes=8 << 20),
+        name="first_final",
+    )(*[held(v) for v in streams[:HALF]], held(lane_mat), held(high_mat))
+    out = pl.pallas_call(
+        second_final_kernel,
+        out_shape=out_shape,
+        in_specs=[vmem] * (HALF + 2) + [hbm],
+        out_specs=hbm,
+        scratch_shapes=scratch,
+        input_output_aliases={HALF + 2: 0},
+        compiler_params=pltpu.CompilerParams(vmem_limit_bytes=8 << 20),
+        name="second_final",
+    )(*[held(v) for v in streams[HALF:]], held(lane_mat), held(high_mat), out)
     return out.reshape(2048, 2, 128).transpose(1, 0, 2).reshape(2, 262144)
 
 

time: 95.3 us -> 107 us (1.12)
  waiting for transfers between devices: 18.3 us -> 43.1 us
  starting transfers between devices: 65 us -> 53.3 us
    ppermute x36, waiting for transfers between devices: 17.5 us -> 42.2 us  [shards(): got = lax.ppermute(streams[i], AXES, pairs_of('xyz'[k], first))]
    ppermute x36, starting transfers between devices: 63.7 us -> 52 us  [shards(): got = lax.ppermute(streams[i], AXES, pairs_of('xyz'[k], first))]
    pallas_call x2 -> x3, Pallas kernels: 8.88 us -> 7.82 us  [the longest x1 3.99 us: shards(): pl.pallas_call(phase_kernel, out_shape=[pltpu.VMEM(s, F32) for s in SHAPE...]
  transfers between devices with their start and end apart: 42 -> 42, of which waited for: 14 -> 16; matrix products, arithmetic and copies ran while one was open for 2% -> 2% of each run, Pallas kernels for 0% -> 2%
where the time goes in v2:
time: 107 us
  starting transfers between devices  53.3 us (50%)
  waiting for transfers between devices  43.1 us (40%)
  Pallas kernels  7.82 us (7%)
  other arithmetic  2.54 us (2%)
    ppermute x36, starting transfers between devices, shards(): got = lax.ppermute(streams[i], AXES, pairs_of('xyz'[k], first))  52 us
    ppermute x36, waiting for transfers between devices, shards(): got = lax.ppermute(streams[i], AXES, pairs_of('xyz'[k], first))  42.2 us
    pallas_call x1, Pallas kernels, shards(): pl.pallas_call(phase_kernel, out_shape=[pltpu.VMEM(s, F32) for s in SHAPE...  3.99 us
  transfers between devices with their start and end apart: 42, of which 16 were waited for; matrix products, arithmetic and copies ran while one was open for 2% of the time, Pallas kernels for 2%

profile of v2, /device:TPU:0, one launch (start us, length us, event | category | flops | bytes accessed | tf_op | source)
XLA Modules:
  0.0 107.3 jit_solution(12002701442366344118)
XLA Ops:
  0.0 4.0 %phase_step.1 = (f32[688,128]{1,0:T(8,128)S(1)}, f32[680,128]{1,0:T(8,128)S(1)}, f32[85,8,128]{2,1,0:T(8,128)S(1)}, f32[43,16,128]{2,1,0:T(8,128)S(1)}, f32[5,13...) custom-call(f32[4096,128]{1,0:T(8,128)} %bitcast.30, ...), custom_call_target="tpu_custom_call" | custom-call | tf_op jit(solution)/shard_map/phase_step/pallas_call | solution.py:260
  8.0 2.0 %collective-permute-start.15 = (f32[17,40,128]{2,1,0:T(8,128)S(1)}, f32[17,40,128]{2,1,0:T(8,128)S(1)}, u32[]{:S(2)}, u32[]{:S(2)}) collective-permute-start(f32[17,40,128]{2,1,0:T(8,128)S(1)} %multiply_add_fusion.19), channel_id=1, source_target_pairs={{0,32},{1,33},{2,34},{3,35},{4,36},{5,37},{6,38},{7,39},{8,40},{9,... | collective-permute-start | bytes 1044488 | tf_op jit(solution)/shard_map/ppermute | solution.py:279
  15.4 2.9 %collective-permute-start.9 = (f32[5,136,128]{2,1,0:T(8,128)S(1)}, f32[5,136,128]{2,1,0:T(8,128)S(1)}, u32[]{:S(2)}, u32[]{:S(2)}) collective-permute-start(f32[5,136,128]{2,1,0:T(8,128)S(1)} %multiply_add_fusion.22), channel_id=1, source_target_pairs={{0,6},{1,7},{2,4},{3,5},{4,2},{5,3},{6,0},{7,1},{8,14},{9,15},{10,... | collective-permute-start | bytes 1044488 | tf_op jit(solution)/shard_map/ppermute | solution.py:279
  18.3 4.1 %collective-permute-start.16 = (f32[17,40,128]{2,1,0:T(8,128)S(1)}, f32[17,40,128]{2,1,0:T(8,128)S(1)}, u32[]{:S(2)}, u32[]{:S(2)}) collective-permute-start(f32[17,40,128]{2,1,0:T(8,128)S(1)} %multiply_add_fusion.18), channel_id=1, source_target_pairs={{0,96},{1,97},{2,98},{3,99},{4,100},{5,101},{6,102},{7,103},{8,104... | collective-permute-start | bytes 1044488 | tf_op jit(solution)/shard_map/ppermute | solution.py:279
  22.5 2.0 %collective-permute-start.30 = (f32[680,128]{1,0:T(8,128)S(1)}, f32[680,128]{1,0:T(8,128)S(1)}, u32[]{:S(2)}, u32[]{:S(2)}) collective-permute-start(f32[680,128]{1,0:T(8,128)S(1)} %multiply_add_fusion.14), channel_id=1, source_target_pairs={{0,6},{1,7},{2,4},{3,5},{4,2},{5,3},{6,0},{7,1},{8,14},{9,15},{10,... | collective-permute-start | bytes 1044488 | tf_op jit(solution)/shard_map/ppermute | solution.py:279
  25.5 2.8 %collective-permute-start.2 = (f32[43,16,128]{2,1,0:T(8,128)S(1)}, f32[43,16,128]{2,1,0:T(8,128)S(1)}, u32[]{:S(2)}, u32[]{:S(2)}) collective-permute-start(f32[43,16,128]{2,1,0:T(8,128)S(1)} %multiply_add_fusion.6), channel_id=1, source_target_pairs={{0,9},{1,8},{2,11},{3,10},{4,13},{5,12},{6,15},{7,14},{8,1},{9,0},... | collective-permute-start | bytes 1056776 | tf_op jit(solution)/shard_map/ppermute | solution.py:279
  31.9 2.6 %collective-permute-done.37 = f32[85,8,128]{2,1,0:T(8,128)S(1)} collective-permute-done((f32[85,8,128]{2,1,0:T(8,128)S(1)}, f32[85,8,128]{2,1,0:T(8,128)S(1)}, u32[]{:S(2)}, u32[]{:S(2)}) %collective-permute-start.37) | collective-permute-done | bytes 348192 | tf_op jit(solution)/shard_map/ppermute | solution.py:279
  36.3 5.7 %collective-permute-done.23 = f32[688,128]{1,0:T(8,128)S(1)} collective-permute-done((f32[688,128]{1,0:T(8,128)S(1)}, f32[688,128]{1,0:T(8,128)S(1)}, u32[]{:S(2)}, u32[]{:S(2)}) %collective-permute-start.23) | collective-permute-done | bytes 352288 | tf_op jit(solution)/shard_map/ppermute | solution.py:279
  44.3 3.8 %collective-permute-start.11 = (f32[5,136,128]{2,1,0:T(8,128)S(1)}, f32[5,136,128]{2,1,0:T(8,128)S(1)}, u32[]{:S(2)}, u32[]{:S(2)}) collective-permute-start(f32[5,136,128]{2,1,0:T(8,128)S(1)} %multiply_add_fusion.21), channel_id=1, source_target_pairs={{0,96},{1,97},{2,98},{3,99},{4,100},{5,101},{6,102},{7,103},{8,104... | collective-permute-start | bytes 1044488 | tf_op jit(solution)/shard_map/ppermute | solution.py:279
  48.2 2.8 %collective-permute-start.18 = (f32[17,40,128]{2,1,0:T(8,128)S(1)}, f32[17,40,128]{2,1,0:T(8,128)S(1)}, u32[]{:S(2)}, u32[]{:S(2)}) collective-permute-start(f32[17,40,128]{2,1,0:T(8,128)S(1)} %multiply_add_fusion.17), channel_id=1, source_target_pairs={{0,9},{1,8},{2,11},{3,10},{4,13},{5,12},{6,15},{7,14},{8,1},{9,0},... | collective-permute-start | bytes 1044488 | tf_op jit(solution)/shard_map/ppermute | solution.py:279
  52.2 3.2 %collective-permute-done.24 = f32[688,128]{1,0:T(8,128)S(1)} collective-permute-done((f32[688,128]{1,0:T(8,128)S(1)}, f32[688,128]{1,0:T(8,128)S(1)}, u32[]{:S(2)}, u32[]{:S(2)}) %collective-permute-start.24) | collective-permute-done | bytes 352288 | tf_op jit(solution)/shard_map/ppermute | solution.py:279
  55.4 3.5 %collective-permute-start.25 = (f32[688,128]{1,0:T(8,128)S(1)}, f32[688,128]{1,0:T(8,128)S(1)}, u32[]{:S(2)}, u32[]{:S(2)}) collective-permute-start(f32[688,128]{1,0:T(8,128)S(1)} %multiply_add_fusion.1), channel_id=1, source_target_pairs={{0,6},{1,7},{2,4},{3,5},{4,2},{5,3},{6,0},{7,1},{8,14},{9,15},{10,... | collective-permute-start | bytes 1056776 | tf_op jit(solution)/shard_map/ppermute | solution.py:279
  59.0 2.4 %collective-permute-start.12 = (f32[5,136,128]{2,1,0:T(8,128)S(1)}, f32[5,136,128]{2,1,0:T(8,128)S(1)}, u32[]{:S(2)}, u32[]{:S(2)}) collective-permute-start(f32[5,136,128]{2,1,0:T(8,128)S(1)} %add_add_fusion.16), channel_id=1, source_target_pairs={{0,8},{1,9},{2,10},{3,11},{4,12},{5,13},{6,14},{7,15},{8,0},{9,1},... | collective-permute-start | bytes 1044488 | tf_op jit(solution)/shard_map/ppermute | solution.py:279
  62.4 3.9 %collective-permute-done.39 = f32[85,8,128]{2,1,0:T(8,128)S(1)} collective-permute-done((f32[85,8,128]{2,1,0:T(8,128)S(1)}, f32[85,8,128]{2,1,0:T(8,128)S(1)}, u32[]{:S(2)}, u32[]{:S(2)}) %collective-permute-start.39) | collective-permute-done | bytes 348192 | tf_op jit(solution)/shard_map/ppermute | solution.py:279
  68.4 4.0 %collective-permute-done.25 = f32[688,128]{1,0:T(8,128)S(1)} collective-permute-done((f32[688,128]{1,0:T(8,128)S(1)}, f32[688,128]{1,0:T(8,128)S(1)}, u32[]{:S(2)}, u32[]{:S(2)}) %collective-permute-start.25) | collective-permute-done | bytes 352288 | tf_op jit(solution)/shard_map/ppermute | solution.py:279
  72.6 2.1 %collective-permute-start.26 = (f32[688,128]{1,0:T(8,128)S(1)}, f32[688,128]{1,0:T(8,128)S(1)}, u32[]{:S(2)}, u32[]{:S(2)}) collective-permute-start(f32[688,128]{1,0:T(8,128)S(1)} %add_add_fusion.1), channel_id=1, source_target_pairs={{0,32},{1,33},{2,34},{3,35},{4,36},{5,37},{6,38},{7,39},{8,40},{9,... | collective-permute-start | bytes 1056776 | tf_op jit(solution)/shard_map/ppermute | solution.py:279
  78.7 1.9 %collective-permute-start.34 = (f32[680,128]{1,0:T(8,128)S(1)}, f32[680,128]{1,0:T(8,128)S(1)}, u32[]{:S(2)}, u32[]{:S(2)}) collective-permute-start(f32[680,128]{1,0:T(8,128)S(1)} %multiply_add_fusion.12), channel_id=1, source_target_pairs={{0,9},{1,8},{2,11},{3,10},{4,13},{5,12},{6,15},{7,14},{8,1},{9,0},... | collective-permute-start | bytes 1044488 | tf_op jit(solution)/shard_map/ppermute | solution.py:279
  80.6 3.0 %collective-permute-done.5 = f32[43,16,128]{2,1,0:T(8,128)S(1)} collective-permute-done((f32[43,16,128]{2,1,0:T(8,128)S(1)}, f32[43,16,128]{2,1,0:T(8,128)S(1)}, u32[]{:S(2)}, u32[]{:S(2)}) %collective-permute-start.5) | collective-permute-done | bytes 352288 | tf_op jit(solution)/shard_map/ppermute | solution.py:279
  83.6 2.2 %collective-permute-start.41 = (f32[85,8,128]{2,1,0:T(8,128)S(1)}, f32[85,8,128]{2,1,0:T(8,128)S(1)}, u32[]{:S(2)}, u32[]{:S(2)}) collective-permute-start(f32[85,8,128]{2,1,0:T(8,128)S(1)} %multiply_add_fusion.8), channel_id=1, source_target_pairs={{0,6},{1,7},{2,4},{3,5},{4,2},{5,3},{6,0},{7,1},{8,14},{9,15},{10,... | collective-permute-start | bytes 1044488 | tf_op jit(solution)/shard_map/ppermute | solution.py:279
  85.8 4.6 %collective-permute-done.26 = f32[688,128]{1,0:T(8,128)S(1)} collective-permute-done((f32[688,128]{1,0:T(8,128)S(1)}, f32[688,128]{1,0:T(8,128)S(1)}, u32[]{:S(2)}, u32[]{:S(2)}) %collective-permute-start.26) | collective-permute-done | bytes 352288 | tf_op jit(solution)/shard_map/ppermute | solution.py:279
  90.4 3.6 %collective-permute-start.6 = (f32[43,16,128]{2,1,0:T(8,128)S(1)}, f32[43,16,128]{2,1,0:T(8,128)S(1)}, u32[]{:S(2)}, u32[]{:S(2)}) collective-permute-start(f32[43,16,128]{2,1,0:T(8,128)S(1)} %multiply_add_fusion.4), channel_id=1, source_target_pairs={{0,96},{1,97},{2,98},{3,99},{4,100},{5,101},{6,102},{7,103},{8,104... | collective-permute-start | bytes 1056776 | tf_op jit(solution)/shard_map/ppermute | solution.py:279
  94.6 8.6 %collective-permute-done.27 = f32[688,128]{1,0:T(8,128)S(1)} collective-permute-done((f32[688,128]{1,0:T(8,128)S(1)}, f32[688,128]{1,0:T(8,128)S(1)}, u32[]{:S(2)}, u32[]{:S(2)}) %collective-permute-start.27) | collective-permute-done | bytes 352288 | tf_op jit(solution)/shard_map/ppermute | solution.py:279
  103.3 1.9 %first_final.1.refs_5_ = f32[128,32,128]{2,1,0:T(8,128)} custom-call(f32[688,128]{1,0:T(8,128)S(1)} %add_add_fusion.refs_0_, f32[680,128]{1,0:T(8,128)S(1)} %add_add_fusion.9.refs_1_, f32[85,8,128]{2,1,0:T(8,128)S(1)} %add_add_fusion.6.refs_2_, bf16[256,256]{1,0:T(8,128)(2,1)S(1)} %get-tuple-element.18.refs_3_, bf16[128,384]{1,0:T(8,128)(2,1)S(1)} %get-tuple-element.19.refs_4_), custom_call_target="tpu_custom_call" | custom-call | tf_op jit(solution)/shard_map/first_final/pallas_call | solution.py:292
  105.3 1.9 %second_final.1 = f32[128,32,128]{2,1,0:T(8,128)} custom-call(f32[43,16,128]{2,1,0:T(8,128)S(1)} %add_add_fusion.3.refs_0_, f32[5,136,128]{2,1,0:T(8,128)S(1)} %add_add_fusion.15.refs_1_, f32[17,40,128]{2,1,0:T(8,128)S(1)} %add_add_fusion.12.refs_2_, bf16[256,256]{1,0:T(8,128)(2,1)S(1)} %get-tuple-element.18.refs_3_, ...), custom_call_target="tpu_custom_call", output_to_operand_aliasing={{}: (5, {})} | custom-call | tf_op jit(solution)/shard_map/second_final/pallas_call | solution.py:301
  (106 shorter events, 27.1 us)
Async XLA Ops:
  10.7 11.9 %collective-permute-start.36 = (f32[85,8,128]{2,1,0:T(8,128)S(1)}, f32[85,8,128]{2,1,0:T(8,128)S(1)}, u32[]{:S(2)}, u32[]{:S(2)}) collective-permute-start(f32[85,8,128]{2,1,0:T(8,128)S(1)} %multiply_add_fusion.11), channel_id=1, source_target_pairs={{0,32},{1,33},{2,34},{3,35},{4,36},{5,37},{6,38},{7,39},{8,40},{9,... | collective-permute-start | bytes 1044488 | tf_op jit(solution)/shard_map/ppermute | solution.py:279
  11.0 13.6 %collective-permute-start.1 = (f32[43,16,128]{2,1,0:T(8,128)S(1)}, f32[43,16,128]{2,1,0:T(8,128)S(1)}, u32[]{:S(2)}, u32[]{:S(2)}) collective-permute-start(f32[43,16,128]{2,1,0:T(8,128)S(1)} %multiply_add_fusion.7), channel_id=1, source_target_pairs={{0,8},{1,9},{2,10},{3,11},{4,12},{5,13},{6,14},{7,15},{8,0},{9,1},... | collective-permute-start | bytes 1056776 | tf_op jit(solution)/shard_map/ppermute | solution.py:279
  13.5 12.0 %collective-permute-start.22 = (f32[688,128]{1,0:T(8,128)S(1)}, f32[688,128]{1,0:T(8,128)S(1)}, u32[]{:S(2)}, u32[]{:S(2)}) collective-permute-start(f32[688,128]{1,0:T(8,128)S(1)} %multiply_add_fusion.3), channel_id=1, source_target_pairs={{0,8},{1,9},{2,10},{3,11},{4,12},{5,13},{6,14},{7,15},{8,0},{9,1},... | collective-permute-start | bytes 1056776 | tf_op jit(solution)/shard_map/ppermute | solution.py:279
  15.4 13.0 %collective-permute-start.9 = (f32[5,136,128]{2,1,0:T(8,128)S(1)}, f32[5,136,128]{2,1,0:T(8,128)S(1)}, u32[]{:S(2)}, u32[]{:S(2)}) collective-permute-start(f32[5,136,128]{2,1,0:T(8,128)S(1)} %multiply_add_fusion.22), channel_id=1, source_target_pairs={{0,6},{1,7},{2,4},{3,5},{4,2},{5,3},{6,0},{7,1},{8,14},{9,15},{10,... | collective-permute-start | bytes 1044488 | tf_op jit(solution)/shard_map/ppermute | solution.py:279
  28.4 13.6 %collective-permute-start.23 = (f32[688,128]{1,0:T(8,128)S(1)}, f32[688,128]{1,0:T(8,128)S(1)}, u32[]{:S(2)}, u32[]{:S(2)}) collective-permute-start(f32[688,128]{1,0:T(8,128)S(1)} %multiply_add_fusion.2), channel_id=1, source_target_pairs={{0,9},{1,8},{2,11},{3,10},{4,13},{5,12},{6,15},{7,14},{8,1},{9,0},... | collective-permute-start | bytes 1056776 | tf_op jit(solution)/shard_map/ppermute | solution.py:279
  29.1 14.3 %collective-permute-start.10 = (f32[5,136,128]{2,1,0:T(8,128)S(1)}, f32[5,136,128]{2,1,0:T(8,128)S(1)}, u32[]{:S(2)}, u32[]{:S(2)}) collective-permute-start(f32[5,136,128]{2,1,0:T(8,128)S(1)} %add_add_fusion.17), channel_id=1, source_target_pairs={{0,32},{1,33},{2,34},{3,35},{4,36},{5,37},{6,38},{7,39},{8,40},{9,... | collective-permute-start | bytes 1044488 | tf_op jit(solution)/shard_map/ppermute | solution.py:279
  31.1 13.2 %collective-permute-start.17 = (f32[17,40,128]{2,1,0:T(8,128)S(1)}, f32[17,40,128]{2,1,0:T(8,128)S(1)}, u32[]{:S(2)}, u32[]{:S(2)}) collective-permute-start(f32[17,40,128]{2,1,0:T(8,128)S(1)} %add_add_fusion.14), channel_id=1, source_target_pairs={{0,8},{1,9},{2,10},{3,11},{4,12},{5,13},{6,14},{7,15},{8,0},{9,1},... | collective-permute-start | bytes 1044488 | tf_op jit(solution)/shard_map/ppermute | solution.py:279
  34.6 13.6 %collective-permute-start.31 = (f32[680,128]{1,0:T(8,128)S(1)}, f32[680,128]{1,0:T(8,128)S(1)}, u32[]{:S(2)}, u32[]{:S(2)}) collective-permute-start(f32[680,128]{1,0:T(8,128)S(1)} %add_add_fusion.11), channel_id=1, source_target_pairs={{0,32},{1,33},{2,34},{3,35},{4,36},{5,37},{6,38},{7,39},{8,40},{9,... | collective-permute-start | bytes 1044488 | tf_op jit(solution)/shard_map/ppermute | solution.py:279
  34.7 16.4 %collective-permute-start.38 = (f32[85,8,128]{2,1,0:T(8,128)S(1)}, f32[85,8,128]{2,1,0:T(8,128)S(1)}, u32[]{:S(2)}, u32[]{:S(2)}) collective-permute-start(f32[85,8,128]{2,1,0:T(8,128)S(1)} %add_add_fusion.8), channel_id=1, source_target_pairs={{0,8},{1,9},{2,10},{3,11},{4,12},{5,13},{6,14},{7,15},{8,0},{9,1},... | collective-permute-start | bytes 1044488 | tf_op jit(solution)/shard_map/ppermute | solution.py:279
  43.4 12.0 %collective-permute-start.24 = (f32[688,128]{1,0:T(8,128)S(1)}, f32[688,128]{1,0:T(8,128)S(1)}, u32[]{:S(2)}, u32[]{:S(2)}) collective-permute-start(f32[688,128]{1,0:T(8,128)S(1)} %add_add_fusion.2), channel_id=1, source_target_pairs={{0,2},{1,3},{2,0},{3,1},{4,6},{5,7},{6,4},{7,5},{8,10},{9,11},{10,... | collective-permute-start | bytes 1056776 | tf_op jit(solution)/shard_map/ppermute | solution.py:279
  44.3 11.1 %collective-permute-start.11 = (f32[5,136,128]{2,1,0:T(8,128)S(1)}, f32[5,136,128]{2,1,0:T(8,128)S(1)}, u32[]{:S(2)}, u32[]{:S(2)}) collective-permute-start(f32[5,136,128]{2,1,0:T(8,128)S(1)} %multiply_add_fusion.21), channel_id=1, source_target_pairs={{0,96},{1,97},{2,98},{3,99},{4,100},{5,101},{6,102},{7,103},{8,104... | collective-permute-start | bytes 1044488 | tf_op jit(solution)/shard_map/ppermute | solution.py:279
  51.2 15.1 %collective-permute-start.39 = (f32[85,8,128]{2,1,0:T(8,128)S(1)}, f32[85,8,128]{2,1,0:T(8,128)S(1)}, u32[]{:S(2)}, u32[]{:S(2)}) collective-permute-start(f32[85,8,128]{2,1,0:T(8,128)S(1)} %multiply_add_fusion.9), channel_id=1, source_target_pairs={{0,9},{1,8},{2,11},{3,10},{4,13},{5,12},{6,15},{7,14},{8,1},{9,0},... | collective-permute-start | bytes 1044488 | tf_op jit(solution)/shard_map/ppermute | solution.py:279
  55.4 12.3 %collective-permute-start.4 = (f32[43,16,128]{2,1,0:T(8,128)S(1)}, f32[43,16,128]{2,1,0:T(8,128)S(1)}, u32[]{:S(2)}, u32[]{:S(2)}) collective-permute-start(f32[43,16,128]{2,1,0:T(8,128)S(1)} %multiply_add_fusion.5), channel_id=1, source_target_pairs={{0,6},{1,7},{2,4},{3,5},{4,2},{5,3},{6,0},{7,1},{8,14},{9,15},{10,... | collective-permute-start | bytes 1056776 | tf_op jit(solution)/shard_map/ppermute | solution.py:279
  55.4 17.1 %collective-permute-start.25 = (f32[688,128]{1,0:T(8,128)S(1)}, f32[688,128]{1,0:T(8,128)S(1)}, u32[]{:S(2)}, u32[]{:S(2)}) collective-permute-start(f32[688,128]{1,0:T(8,128)S(1)} %multiply_add_fusion.1), channel_id=1, source_target_pairs={{0,6},{1,7},{2,4},{3,5},{4,2},{5,3},{6,0},{7,1},{8,14},{9,15},{10,... | collective-permute-start | bytes 1056776 | tf_op jit(solution)/shard_map/ppermute | solution.py:279
  59.0 13.6 %collective-permute-start.12 = (f32[5,136,128]{2,1,0:T(8,128)S(1)}, f32[5,136,128]{2,1,0:T(8,128)S(1)}, u32[]{:S(2)}, u32[]{:S(2)}) collective-permute-start(f32[5,136,128]{2,1,0:T(8,128)S(1)} %add_add_fusion.16), channel_id=1, source_target_pairs={{0,8},{1,9},{2,10},{3,11},{4,12},{5,13},{6,14},{7,15},{8,0},{9,1},... | collective-permute-start | bytes 1044488 | tf_op jit(solution)/shard_map/ppermute | solution.py:279
  61.5 13.3 %collective-permute-start.19 = (f32[17,40,128]{2,1,0:T(8,128)S(1)}, f32[17,40,128]{2,1,0:T(8,128)S(1)}, u32[]{:S(2)}, u32[]{:S(2)}) collective-permute-start(f32[17,40,128]{2,1,0:T(8,128)S(1)} %add_add_fusion.13), channel_id=1, source_target_pairs={{0,2},{1,3},{2,0},{3,1},{4,6},{5,7},{6,4},{7,5},{8,10},{9,11},{10,... | collective-permute-start | bytes 1044488 | tf_op jit(solution)/shard_map/ppermute | solution.py:279
  66.3 11.0 %collective-permute-start.33 = (f32[680,128]{1,0:T(8,128)S(1)}, f32[680,128]{1,0:T(8,128)S(1)}, u32[]{:S(2)}, u32[]{:S(2)}) collective-permute-start(f32[680,128]{1,0:T(8,128)S(1)} %add_add_fusion.10), channel_id=1, source_target_pairs={{0,8},{1,9},{2,10},{3,11},{4,12},{5,13},{6,14},{7,15},{8,0},{9,1},... | collective-permute-start | bytes 1044488 | tf_op jit(solution)/shard_map/ppermute | solution.py:279
  67.7 11.0 %collective-permute-start.40 = (f32[85,8,128]{2,1,0:T(8,128)S(1)}, f32[85,8,128]{2,1,0:T(8,128)S(1)}, u32[]{:S(2)}, u32[]{:S(2)}) collective-permute-start(f32[85,8,128]{2,1,0:T(8,128)S(1)} %add_add_fusion.7), channel_id=1, source_target_pairs={{0,2},{1,3},{2,0},{3,1},{4,6},{5,7},{6,4},{7,5},{8,10},{9,11},{10,... | collective-permute-start | bytes 1044488 | tf_op jit(solution)/shard_map/ppermute | solution.py:279
  72.5 11.1 %collective-permute-start.5 = (f32[43,16,128]{2,1,0:T(8,128)S(1)}, f32[43,16,128]{2,1,0:T(8,128)S(1)}, u32[]{:S(2)}, u32[]{:S(2)}) collective-permute-start(f32[43,16,128]{2,1,0:T(8,128)S(1)} %add_add_fusion.4), channel_id=1, source_target_pairs={{0,32},{1,33},{2,34},{3,35},{4,36},{5,37},{6,38},{7,39},{8,40},{9,... | collective-permute-start | bytes 1056776 | tf_op jit(solution)/shard_map/ppermute | solution.py:279
  72.6 17.8 %collective-permute-start.26 = (f32[688,128]{1,0:T(8,128)S(1)}, f32[688,128]{1,0:T(8,128)S(1)}, u32[]{:S(2)}, u32[]{:S(2)}) collective-permute-start(f32[688,128]{1,0:T(8,128)S(1)} %add_add_fusion.1), channel_id=1, source_target_pairs={{0,32},{1,33},{2,34},{3,35},{4,36},{5,37},{6,38},{7,39},{8,40},{9,... | collective-permute-start | bytes 1056776 | tf_op jit(solution)/shard_map/ppermute | solution.py:279
  74.8 19.4 %collective-permute-start.13 = (f32[5,136,128]{2,1,0:T(8,128)S(1)}, f32[5,136,128]{2,1,0:T(8,128)S(1)}, u32[]{:S(2)}, u32[]{:S(2)}) collective-permute-start(f32[5,136,128]{2,1,0:T(8,128)S(1)} %multiply_add_fusion.20), channel_id=1, source_target_pairs={{0,9},{1,8},{2,11},{3,10},{4,13},{5,12},{6,15},{7,14},{8,1},{9,0},... | collective-permute-start | bytes 1044488 | tf_op jit(solution)/shard_map/ppermute | solution.py:279
  77.4 17.0 %collective-permute-start.20 = (f32[17,40,128]{2,1,0:T(8,128)S(1)}, f32[17,40,128]{2,1,0:T(8,128)S(1)}, u32[]{:S(2)}, u32[]{:S(2)}) collective-permute-start(f32[17,40,128]{2,1,0:T(8,128)S(1)} %multiply_add_fusion.16), channel_id=1, source_target_pairs={{0,6},{1,7},{2,4},{3,5},{4,2},{5,3},{6,0},{7,1},{8,14},{9,15},{10,... | collective-permute-start | bytes 1044488 | tf_op jit(solution)/shard_map/ppermute | solution.py:279
  78.7 15.7 %collective-permute-start.34 = (f32[680,128]{1,0:T(8,128)S(1)}, f32[680,128]{1,0:T(8,128)S(1)}, u32[]{:S(2)}, u32[]{:S(2)}) collective-permute-start(f32[680,128]{1,0:T(8,128)S(1)} %multiply_add_fusion.12), channel_id=1, source_target_pairs={{0,9},{1,8},{2,11},{3,10},{4,13},{5,12},{6,15},{7,14},{8,1},{9,0},... | collective-permute-start | bytes 1044488 | tf_op jit(solution)/shard_map/ppermute | solution.py:279
  90.4 14.7 %collective-permute-start.6 = (f32[43,16,128]{2,1,0:T(8,128)S(1)}, f32[43,16,128]{2,1,0:T(8,128)S(1)}, u32[]{:S(2)}, u32[]{:S(2)}) collective-permute-start(f32[43,16,128]{2,1,0:T(8,128)S(1)} %multiply_add_fusion.4), channel_id=1, source_target_pairs={{0,96},{1,97},{2,98},{3,99},{4,100},{5,101},{6,102},{7,103},{8,104... | collective-permute-start | bytes 1056776 | tf_op jit(solution)/shard_map/ppermute | solution.py:279
  (18 other events, 135.2 us)

commit v3 on v2

--- a/solution.py
+++ b/solution.py
@@ -9,7 +9,7 @@
 AXES = ("gx", "gy", "gz")
 SHAPES = ((688, 128), (680, 128), (85, 8, 128), (43, 16, 128), (5, 136, 128), (17, 40, 128))
 ROWS = (688, 680, 680, 688, 680, 680)
-FIRST_DIM = (0, 1, 2, 0, 1, 2)
+FIRST_DIM = (0, 1, 2, 1, 2, 0)
 COUNT = len(SHAPES)
 HALF = COUNT // 2
 BASES = tuple(sum(ROWS[:i]) for i in range(COUNT))
@@ -97,7 +97,7 @@
 
 
 def phase_kernel(x_hbm, j_ref, f_ref, *refs):
-    outs, (coef_ref, lane_ref, high_ref, x_ref, sems) = refs[:COUNT], refs[COUNT:]
+    outs, (coef_ref, tan_ref, x_ref, sems) = refs[:COUNT], refs[COUNT:]
     copies = [
         pltpu.make_async_copy(x_hbm.at[pl.ds(1024 * h, 1024), :], x_ref.at[pl.ds(1024 * h, 1024), :], sems.at[h])
         for h in range(4)
@@ -157,15 +157,7 @@
         [jnp.transpose(jnp.broadcast_to(e[v : v + 1, :], (128, 128))) for e in (e2r, e2i)] for v in range(2)
     ]
 
-    lane_hi, lane_lo = split(rotation(tangents, 0, True))
-    lane_ref[0:128, 0:128] = lane_hi
-    lane_ref[0:128, 128:256] = lane_lo
-    lane_ref[128:256, 0:128] = lane_hi
-    lane_ref[128:256, 128:256] = jnp.zeros((128, 128), BF16)
-    high_hi, high_lo = split(rotation(tangents, 11, False))
-    high_ref[:, 0:128] = high_hi
-    high_ref[:, 128:256] = high_lo
-    high_ref[:, 256:384] = high_hi
+    tan_ref[...] = tangents
 
     low_tangents = [jnp.broadcast_to(tangents[7 + k : 8 + k, :], (8, 128)) for k in range(4)]
     for at in range(0, 128, 8):
@@ -193,7 +185,7 @@
                 ref[index] = v[rl]
 
 
-def finish(ins, base, lane_ref, high_ref, out_hbm, o_ref, sems):
+def finish(ins, base, first, last, lane_ref, high_ref, out_hbm, o_ref, sems):
     number = device_bits()
     device_ones = number & 1
     for k in range(1, 7):
@@ -201,7 +193,7 @@
     rows = lax.broadcasted_iota(jnp.int32, (128, 128), 0)
     cols = lax.broadcasted_iota(jnp.int32, (128, 128), 1)
     turns = ones_in(rows, 7) + ones_in(cols, 7) + device_ones
-    first = 0 if base == 0 else 8
+    width = 2 * (last - first)
 
     def read(row):
         parts = []
@@ -211,7 +203,7 @@
         return jnp.concatenate(parts, axis=0)
 
     copies = []
-    for rl in range(first, first + 8):
+    for rl in range(first, last):
         y = jnp.concatenate([read(rl * 256), read(rl * 256 + 128)], axis=0)
         y_hi, y_lo = split(y)
         p = jnp.dot(jnp.concatenate([y_hi, y_lo], axis=1), lane_ref[...], preferred_element_type=F32)
@@ -224,13 +216,13 @@
         out_re = jnp.where(odd, im, re)
         out_im = jnp.where(odd, re, im)
         at = 2 * (rl - first)
-        o_ref[pl.ds(at, 128, stride=16), :] = jnp.where(quarter >= 2, -out_re, out_re)
-        o_ref[pl.ds(at + 1, 128, stride=16), :] = jnp.where((quarter == 1) | (quarter == 2), -out_im, out_im)
+        o_ref[pl.ds(at, 128, stride=width), :] = jnp.where(quarter >= 2, -out_re, out_re)
+        o_ref[pl.ds(at + 1, 128, stride=width), :] = jnp.where((quarter == 1) | (quarter == 2), -out_im, out_im)
         if rl % 4 == 3:
             part = (rl - first) // 4
             copies.append(
                 pltpu.make_async_copy(
-                    o_ref.reshape(128, 16, 128).at[:, pl.ds(8 * part, 8), :],
+                    o_ref.reshape(128, width, 128).at[:, pl.ds(8 * part, 8), :],
                     out_hbm.at[:, pl.ds(2 * first + 8 * part, 8), :],
                     sems.at[part],
                 )
@@ -241,11 +233,22 @@
 
 
 def first_final_kernel(*refs):
-    finish(refs[:HALF], 0, *refs[HALF:])
+    ins, (tan_ref, out_hbm, lane_ref, high_ref, o_ref, sems) = refs[:HALF], refs[HALF:]
+    tangents = tan_ref[...]
+    lane_hi, lane_lo = split(rotation(tangents, 0, True))
+    lane_ref[0:128, 0:128] = lane_hi
+    lane_ref[0:128, 128:256] = lane_lo
+    lane_ref[128:256, 0:128] = lane_hi
+    lane_ref[128:256, 128:256] = jnp.zeros((128, 128), BF16)
+    high_hi, high_lo = split(rotation(tangents, 11, False))
+    high_ref[:, 0:128] = high_hi
+    high_ref[:, 128:256] = high_lo
+    high_ref[:, 256:384] = high_hi
+    finish(ins, 0, 0, 8, lane_ref, high_ref, out_hbm, o_ref, sems)
 
 
 def second_final_kernel(*refs):
-    finish(refs[:HALF], HALF, refs[HALF], refs[HALF + 1], *refs[HALF + 3 :])
+    finish(refs[:HALF], HALF, 8, 16, refs[HALF], refs[HALF + 1], *refs[HALF + 3 :])
 
 
 def exchange_order():
@@ -260,13 +263,13 @@
     made = pl.pallas_call(
         phase_kernel,
         out_shape=[pltpu.VMEM(s, F32) for s in SHAPES]
-        + [pltpu.VMEM((16, 128), F32), pltpu.VMEM((256, 256), BF16), pltpu.VMEM((128, 384), BF16)],
+        + [pltpu.VMEM((16, 128), F32), pltpu.VMEM((32, 128), F32)],
         in_specs=[hbm, smem, smem],
-        out_specs=[vmem] * (COUNT + 3),
+        out_specs=[vmem] * (COUNT + 2),
         scratch_shapes=[pltpu.VMEM((4096, 128), F32), pltpu.SemaphoreType.DMA((4,))],
         name="phase_step",
     )(rows, couplings, fields)
-    streams, (coef, lane_mat, high_mat) = list(made[:COUNT]), made[COUNT:]
+    streams, (coef, tangents) = list(made[:COUNT]), made[COUNT:]
 
     kept = [None] * COUNT
     for i, step in exchange_order():
@@ -287,25 +290,26 @@
     def held(value):
         return pltpu.with_memory_space_constraint(value, pltpu.VMEM)
 
+    out_shape = jax.ShapeDtypeStruct((128, 32, 128), F32)
     scratch = [pltpu.VMEM((2048, 128), F32), pltpu.SemaphoreType.DMA((2,))]
-    out_shape = jax.ShapeDtypeStruct((128, 32, 128), F32)
-    out = pl.pallas_call(
+    params = pltpu.CompilerParams(vmem_limit_bytes=8 << 20)
+    out, lane_mat, high_mat = pl.pallas_call(
         first_final_kernel,
-        out_shape=out_shape,
-        in_specs=[vmem] * (HALF + 2),
-        out_specs=hbm,
+        out_shape=[out_shape, pltpu.VMEM((256, 256), BF16), pltpu.VMEM((128, 384), BF16)],
+        in_specs=[vmem] * (HALF + 1),
+        out_specs=[hbm, vmem, vmem],
         scratch_shapes=scratch,
-        compiler_params=pltpu.CompilerParams(vmem_limit_bytes=8 << 20),
+        compiler_params=params,
         name="first_final",
-    )(*[held(v) for v in streams[:HALF]], held(lane_mat), held(high_mat))
+    )(*[held(v) for v in streams[:HALF]], held(tangents))
     out = pl.pallas_call(
         second_final_kernel,
         out_shape=out_shape,
         in_specs=[vmem] * (HALF + 2) + [hbm],
         out_specs=hbm,
         scratch_shapes=scratch,
+        compiler_params=params,
         input_output_aliases={HALF + 2: 0},
-        compiler_params=pltpu.CompilerParams(vmem_limit_bytes=8 << 20),
         name="second_final",
     )(*[held(v) for v in streams[HALF:]], held(lane_mat), held(high_mat), out)
     return out.reshape(2048, 2, 128).transpose(1, 0, 2).reshape(2, 262144)

time: 107 us -> 97.4 us (0.910); the launches traced: 107 us -> 95.7 us
  waiting for transfers between devices: 43.1 us -> 31.2 us
    ppermute x36, waiting for transfers between devices: 42.2 us -> 30.3 us  [shards(): got = lax.ppermute(streams[i], AXES, pairs_of('xyz'[k], first))]
  transfers between devices with their start and end apart: 42 -> 42, of which waited for: 16 -> 16; matrix products, arithmetic and copies ran while one was open for 2% -> 3% of each run, Pallas kernels for 2% -> 2%
where the time goes in v3:
time: 97.4 us; the launch traced here: 95.7 us
  starting transfers between devices  53.7 us (55%)
  waiting for transfers between devices  31.2 us (32%)
  Pallas kernels  7.74 us (8%)
  other arithmetic  2.51 us (3%)
    ppermute x36, starting transfers between devices, shards(): got = lax.ppermute(streams[i], AXES, pairs_of('xyz'[k], first))  52.4 us
    ppermute x36, waiting for transfers between devices, shards(): got = lax.ppermute(streams[i], AXES, pairs_of('xyz'[k], first))  30.3 us
    pallas_call x1, Pallas kernels, shards(): pl.pallas_call(phase_kernel, out_shape=[pltpu.VMEM(s, F32) for s in SHAPE...  3.76 us
    pallas_call x1, Pallas kernels, shards(): pl.pallas_call(first_final_kernel, out_shape=[out_shape, pltpu.VMEM((256,...  2.07 us
  transfers between devices with their start and end apart: 42, of which 16 were waited for; matrix products, arithmetic and copies ran while one was open for 3% of the time, Pallas kernels for 2%

profile of v3, /device:TPU:0, one launch (start us, length us, event | category | flops | bytes accessed | tf_op | source)
XLA Modules:
  0.0 95.7 jit_solution(17075497987091548638)
XLA Ops:
  0.0 3.8 %phase_step.1 = (f32[688,128]{1,0:T(8,128)S(1)}, f32[680,128]{1,0:T(8,128)S(1)}, f32[85,8,128]{2,1,0:T(8,128)S(1)}, f32[43,16,128]{2,1,0:T(8,128)S(1)}, f32[5,13...) custom-call(f32[4096,128]{1,0:T(8,128)} %bitcast.30, ...), custom_call_target="tpu_custom_call" | custom-call | tf_op jit(solution)/shard_map/phase_step/pallas_call | solution.py:263
  6.0 2.0 %collective-permute-start.8 = (f32[5,136,128]{2,1,0:T(8,128)S(1)}, f32[5,136,128]{2,1,0:T(8,128)S(1)}, u32[]{:S(2)}, u32[]{:S(2)}) collective-permute-start(f32[5,136,128]{2,1,0:T(8,128)S(1)} %multiply_add_fusion.23), channel_id=1, source_target_pairs={{0,32},{1,33},{2,34},{3,35},{4,36},{5,37},{6,38},{7,39},{8,40},{9,... | collective-permute-start | bytes 1044488 | tf_op jit(solution)/shard_map/ppermute | solution.py:282
  9.7 1.7 %collective-permute-start.29 = (f32[680,128]{1,0:T(8,128)S(1)}, f32[680,128]{1,0:T(8,128)S(1)}, u32[]{:S(2)}, u32[]{:S(2)}) collective-permute-start(f32[680,128]{1,0:T(8,128)S(1)} %multiply_add_fusion.15), channel_id=1, source_target_pairs={{0,2},{1,3},{2,0},{3,1},{4,6},{5,7},{6,4},{7,5},{8,10},{9,11},{10,... | collective-permute-start | bytes 1044488 | tf_op jit(solution)/shard_map/ppermute | solution.py:282
  15.5 3.6 %collective-permute-start.9 = (f32[5,136,128]{2,1,0:T(8,128)S(1)}, f32[5,136,128]{2,1,0:T(8,128)S(1)}, u32[]{:S(2)}, u32[]{:S(2)}) collective-permute-start(f32[5,136,128]{2,1,0:T(8,128)S(1)} %multiply_add_fusion.22), channel_id=1, source_target_pairs={{0,96},{1,97},{2,98},{3,99},{4,100},{5,101},{6,102},{7,103},{8,104... | collective-permute-start | bytes 1044488 | tf_op jit(solution)/shard_map/ppermute | solution.py:282
  19.1 2.2 %collective-permute-start.16 = (f32[17,40,128]{2,1,0:T(8,128)S(1)}, f32[17,40,128]{2,1,0:T(8,128)S(1)}, u32[]{:S(2)}, u32[]{:S(2)}) collective-permute-start(f32[17,40,128]{2,1,0:T(8,128)S(1)} %multiply_add_fusion.18), channel_id=1, source_target_pairs={{0,9},{1,8},{2,11},{3,10},{4,13},{5,12},{6,15},{7,14},{8,1},{9,0},... | collective-permute-start | bytes 1044488 | tf_op jit(solution)/shard_map/ppermute | solution.py:282
  21.4 3.1 %collective-permute-start.30 = (f32[680,128]{1,0:T(8,128)S(1)}, f32[680,128]{1,0:T(8,128)S(1)}, u32[]{:S(2)}, u32[]{:S(2)}) collective-permute-start(f32[680,128]{1,0:T(8,128)S(1)} %multiply_add_fusion.14), channel_id=1, source_target_pairs={{0,6},{1,7},{2,4},{3,5},{4,2},{5,3},{6,0},{7,1},{8,14},{9,15},{10,... | collective-permute-start | bytes 1044488 | tf_op jit(solution)/shard_map/ppermute | solution.py:282
  26.9 1.9 %collective-permute-start.23 = (f32[688,128]{1,0:T(8,128)S(1)}, f32[688,128]{1,0:T(8,128)S(1)}, u32[]{:S(2)}, u32[]{:S(2)}) collective-permute-start(f32[688,128]{1,0:T(8,128)S(1)} %multiply_add_fusion.2), channel_id=1, source_target_pairs={{0,9},{1,8},{2,11},{3,10},{4,13},{5,12},{6,15},{7,14},{8,1},{9,0},... | collective-permute-start | bytes 1056776 | tf_op jit(solution)/shard_map/ppermute | solution.py:282
  30.4 2.7 %collective-permute-done.37 = f32[85,8,128]{2,1,0:T(8,128)S(1)} collective-permute-done((f32[85,8,128]{2,1,0:T(8,128)S(1)}, f32[85,8,128]{2,1,0:T(8,128)S(1)}, u32[]{:S(2)}, u32[]{:S(2)}) %collective-permute-start.37) | collective-permute-done | bytes 348192 | tf_op jit(solution)/shard_map/ppermute | solution.py:282
  35.3 3.9 %collective-permute-done.23 = f32[688,128]{1,0:T(8,128)S(1)} collective-permute-done((f32[688,128]{1,0:T(8,128)S(1)}, f32[688,128]{1,0:T(8,128)S(1)}, u32[]{:S(2)}, u32[]{:S(2)}) %collective-permute-start.23) | collective-permute-done | bytes 352288 | tf_op jit(solution)/shard_map/ppermute | solution.py:282
  39.8 3.4 %collective-permute-start.11 = (f32[5,136,128]{2,1,0:T(8,128)S(1)}, f32[5,136,128]{2,1,0:T(8,128)S(1)}, u32[]{:S(2)}, u32[]{:S(2)}) collective-permute-start(f32[5,136,128]{2,1,0:T(8,128)S(1)} %multiply_add_fusion.21), channel_id=1, source_target_pairs={{0,9},{1,8},{2,11},{3,10},{4,13},{5,12},{6,15},{7,14},{8,1},{9,0},... | collective-permute-start | bytes 1044488 | tf_op jit(solution)/shard_map/ppermute | solution.py:282
  44.6 3.9 %collective-permute-start.32 = (f32[680,128]{1,0:T(8,128)S(1)}, f32[680,128]{1,0:T(8,128)S(1)}, u32[]{:S(2)}, u32[]{:S(2)}) collective-permute-start(f32[680,128]{1,0:T(8,128)S(1)} %multiply_add_fusion.13), channel_id=1, source_target_pairs={{0,96},{1,97},{2,98},{3,99},{4,100},{5,101},{6,102},{7,103},{8,104... | collective-permute-start | bytes 1044488 | tf_op jit(solution)/shard_map/ppermute | solution.py:282
  48.6 2.1 %collective-permute-start.39 = (f32[85,8,128]{2,1,0:T(8,128)S(1)}, f32[85,8,128]{2,1,0:T(8,128)S(1)}, u32[]{:S(2)}, u32[]{:S(2)}) collective-permute-start(f32[85,8,128]{2,1,0:T(8,128)S(1)} %multiply_add_fusion.9), channel_id=1, source_target_pairs={{0,9},{1,8},{2,11},{3,10},{4,13},{5,12},{6,15},{7,14},{8,1},{9,0},... | collective-permute-start | bytes 1044488 | tf_op jit(solution)/shard_map/ppermute | solution.py:282
  50.7 6.0 %collective-permute-start.4 = (f32[43,16,128]{2,1,0:T(8,128)S(1)}, f32[43,16,128]{2,1,0:T(8,128)S(1)}, u32[]{:S(2)}, u32[]{:S(2)}) collective-permute-start(f32[43,16,128]{2,1,0:T(8,128)S(1)} %multiply_add_fusion.5), channel_id=1, source_target_pairs={{0,96},{1,97},{2,98},{3,99},{4,100},{5,101},{6,102},{7,103},{8,104... | collective-permute-start | bytes 1056776 | tf_op jit(solution)/shard_map/ppermute | solution.py:282
  57.0 1.6 %collective-permute-start.12 = (f32[5,136,128]{2,1,0:T(8,128)S(1)}, f32[5,136,128]{2,1,0:T(8,128)S(1)}, u32[]{:S(2)}, u32[]{:S(2)}) collective-permute-start(f32[5,136,128]{2,1,0:T(8,128)S(1)} %add_add_fusion.16), channel_id=1, source_target_pairs={{0,2},{1,3},{2,0},{3,1},{4,6},{5,7},{6,4},{7,5},{8,10},{9,11},{10,... | collective-permute-start | bytes 1044488 | tf_op jit(solution)/shard_map/ppermute | solution.py:282
  59.1 6.8 %collective-permute-done.4 = f32[43,16,128]{2,1,0:T(8,128)S(1)} collective-permute-done((f32[43,16,128]{2,1,0:T(8,128)S(1)}, f32[43,16,128]{2,1,0:T(8,128)S(1)}, u32[]{:S(2)}, u32[]{:S(2)}) %collective-permute-start.4) | collective-permute-done | bytes 352288 | tf_op jit(solution)/shard_map/ppermute | solution.py:282
  65.9 3.1 %collective-permute-done.25 = f32[688,128]{1,0:T(8,128)S(1)} collective-permute-done((f32[688,128]{1,0:T(8,128)S(1)}, f32[688,128]{1,0:T(8,128)S(1)}, u32[]{:S(2)}, u32[]{:S(2)}) %collective-permute-start.25) | collective-permute-done | bytes 352288 | tf_op jit(solution)/shard_map/ppermute | solution.py:282
  71.0 1.6 %collective-permute-start.20 = (f32[17,40,128]{2,1,0:T(8,128)S(1)}, f32[17,40,128]{2,1,0:T(8,128)S(1)}, u32[]{:S(2)}, u32[]{:S(2)}) collective-permute-start(f32[17,40,128]{2,1,0:T(8,128)S(1)} %multiply_add_fusion.16), channel_id=1, source_target_pairs={{0,96},{1,97},{2,98},{3,99},{4,100},{5,101},{6,102},{7,103},{8,104... | collective-permute-start | bytes 1044488 | tf_op jit(solution)/shard_map/ppermute | solution.py:282
  72.7 4.2 %collective-permute-done.40 = f32[85,8,128]{2,1,0:T(8,128)S(1)} collective-permute-done((f32[85,8,128]{2,1,0:T(8,128)S(1)}, f32[85,8,128]{2,1,0:T(8,128)S(1)}, u32[]{:S(2)}, u32[]{:S(2)}) %collective-permute-start.40) | collective-permute-done | bytes 348192 | tf_op jit(solution)/shard_map/ppermute | solution.py:282
  78.4 1.8 %collective-permute-done.5 = f32[43,16,128]{2,1,0:T(8,128)S(1)} collective-permute-done((f32[43,16,128]{2,1,0:T(8,128)S(1)}, f32[43,16,128]{2,1,0:T(8,128)S(1)}, u32[]{:S(2)}, u32[]{:S(2)}) %collective-permute-start.5) | collective-permute-done | bytes 352288 | tf_op jit(solution)/shard_map/ppermute | solution.py:282
  81.5 4.5 %collective-permute-start.27 = (f32[688,128]{1,0:T(8,128)S(1)}, f32[688,128]{1,0:T(8,128)S(1)}, u32[]{:S(2)}, u32[]{:S(2)}) collective-permute-start(f32[688,128]{1,0:T(8,128)S(1)} %multiply_add_fusion), channel_id=1, source_target_pairs={{0,96},{1,97},{2,98},{3,99},{4,100},{5,101},{6,102},{7,103},{8,104... | collective-permute-start | bytes 1056776 | tf_op jit(solution)/shard_map/ppermute | solution.py:282
  86.3 2.4 %collective-permute-done.41 = f32[85,8,128]{2,1,0:T(8,128)S(1)} collective-permute-done((f32[85,8,128]{2,1,0:T(8,128)S(1)}, f32[85,8,128]{2,1,0:T(8,128)S(1)}, u32[]{:S(2)}, u32[]{:S(2)}) %collective-permute-start.41) | collective-permute-done | bytes 348192 | tf_op jit(solution)/shard_map/ppermute | solution.py:282
  88.7 2.6 %collective-permute-done.27 = f32[688,128]{1,0:T(8,128)S(1)} collective-permute-done((f32[688,128]{1,0:T(8,128)S(1)}, f32[688,128]{1,0:T(8,128)S(1)}, u32[]{:S(2)}, u32[]{:S(2)}) %collective-permute-start.27) | collective-permute-done | bytes 352288 | tf_op jit(solution)/shard_map/ppermute | solution.py:282
  91.5 2.1 %first_final.1 = (f32[128,32,128]{2,1,0:T(8,128)}, bf16[256,256]{1,0:T(8,128)(2,1)S(1)}, bf16[128,384]{1,0:T(8,128)(2,1)S(1)}) custom-call(f32[688,128]{1,0:T(8,128)S(1)} %add_add_fusion.refs_0_, f32[680,128]{1,0:T(8,128)S(1)} %add_add_fusion.9.refs_1_, f32[85,8,128]{2,1,0:T(8,128)S(1)} %add_add_fusion.6.refs_2_, f32[32,128]{1,0:T(8,128)S(1)} %get-tuple-element.23.refs_3_), custom_call_target="tpu_custom_call" | custom-call | tf_op jit(solution)/shard_map/first_final/pallas_call | solution.py:296
  93.6 1.9 %second_final.1 = f32[128,32,128]{2,1,0:T(8,128)} custom-call(f32[43,16,128]{2,1,0:T(8,128)S(1)} %add_add_fusion.3.refs_0_, f32[5,136,128]{2,1,0:T(8,128)S(1)} %add_add_fusion.15.refs_1_, f32[17,40,128]{2,1,0:T(8,128)S(1)} %add_add_fusion.12.refs_2_, bf16[256,256]{1,0:T(8,128)(2,1)S(1)} %get-tuple-element.24.refs_3_, ...), custom_call_target="tpu_custom_call", output_to_operand_aliasing={{}: (5, {})} | custom-call | tf_op jit(solution)/shard_map/second_final/pallas_call | solution.py:305
  (106 shorter events, 22.3 us)
Async XLA Ops:
  11.5 9.9 %collective-permute-start.36 = (f32[85,8,128]{2,1,0:T(8,128)S(1)}, f32[85,8,128]{2,1,0:T(8,128)S(1)}, u32[]{:S(2)}, u32[]{:S(2)}) collective-permute-start(f32[85,8,128]{2,1,0:T(8,128)S(1)} %multiply_add_fusion.11), channel_id=1, source_target_pairs={{0,32},{1,33},{2,34},{3,35},{4,36},{5,37},{6,38},{7,39},{8,40},{9,... | collective-permute-start | bytes 1044488 | tf_op jit(solution)/shard_map/ppermute | solution.py:282
  12.0 12.6 %collective-permute-start.1 = (f32[43,16,128]{2,1,0:T(8,128)S(1)}, f32[43,16,128]{2,1,0:T(8,128)S(1)}, u32[]{:S(2)}, u32[]{:S(2)}) collective-permute-start(f32[43,16,128]{2,1,0:T(8,128)S(1)} %multiply_add_fusion.7), channel_id=1, source_target_pairs={{0,2},{1,3},{2,0},{3,1},{4,6},{5,7},{6,4},{7,5},{8,10},{9,11},{10,... | collective-permute-start | bytes 1056776 | tf_op jit(solution)/shard_map/ppermute | solution.py:282
  13.3 11.8 %collective-permute-start.22 = (f32[688,128]{1,0:T(8,128)S(1)}, f32[688,128]{1,0:T(8,128)S(1)}, u32[]{:S(2)}, u32[]{:S(2)}) collective-permute-start(f32[688,128]{1,0:T(8,128)S(1)} %multiply_add_fusion.3), channel_id=1, source_target_pairs={{0,8},{1,9},{2,10},{3,11},{4,12},{5,13},{6,14},{7,15},{8,0},{9,1},... | collective-permute-start | bytes 1056776 | tf_op jit(solution)/shard_map/ppermute | solution.py:282
  15.5 11.5 %collective-permute-start.9 = (f32[5,136,128]{2,1,0:T(8,128)S(1)}, f32[5,136,128]{2,1,0:T(8,128)S(1)}, u32[]{:S(2)}, u32[]{:S(2)}) collective-permute-start(f32[5,136,128]{2,1,0:T(8,128)S(1)} %multiply_add_fusion.22), channel_id=1, source_target_pairs={{0,96},{1,97},{2,98},{3,99},{4,100},{5,101},{6,102},{7,103},{8,104... | collective-permute-start | bytes 1044488 | tf_op jit(solution)/shard_map/ppermute | solution.py:282
  26.9 12.2 %collective-permute-start.23 = (f32[688,128]{1,0:T(8,128)S(1)}, f32[688,128]{1,0:T(8,128)S(1)}, u32[]{:S(2)}, u32[]{:S(2)}) collective-permute-start(f32[688,128]{1,0:T(8,128)S(1)} %multiply_add_fusion.2), channel_id=1, source_target_pairs={{0,9},{1,8},{2,11},{3,10},{4,13},{5,12},{6,15},{7,14},{8,1},{9,0},... | collective-permute-start | bytes 1056776 | tf_op jit(solution)/shard_map/ppermute | solution.py:282
  28.9 10.4 %collective-permute-start.10 = (f32[5,136,128]{2,1,0:T(8,128)S(1)}, f32[5,136,128]{2,1,0:T(8,128)S(1)}, u32[]{:S(2)}, u32[]{:S(2)}) collective-permute-start(f32[5,136,128]{2,1,0:T(8,128)S(1)} %add_add_fusion.17), channel_id=1, source_target_pairs={{0,8},{1,9},{2,10},{3,11},{4,12},{5,13},{6,14},{7,15},{8,0},{9,1},... | collective-permute-start | bytes 1044488 | tf_op jit(solution)/shard_map/ppermute | solution.py:282
  33.1 10.1 %collective-permute-start.31 = (f32[680,128]{1,0:T(8,128)S(1)}, f32[680,128]{1,0:T(8,128)S(1)}, u32[]{:S(2)}, u32[]{:S(2)}) collective-permute-start(f32[680,128]{1,0:T(8,128)S(1)} %add_add_fusion.11), channel_id=1, source_target_pairs={{0,32},{1,33},{2,34},{3,35},{4,36},{5,37},{6,38},{7,39},{8,40},{9,... | collective-permute-start | bytes 1044488 | tf_op jit(solution)/shard_map/ppermute | solution.py:282
  33.7 10.8 %collective-permute-start.38 = (f32[85,8,128]{2,1,0:T(8,128)S(1)}, f32[85,8,128]{2,1,0:T(8,128)S(1)}, u32[]{:S(2)}, u32[]{:S(2)}) collective-permute-start(f32[85,8,128]{2,1,0:T(8,128)S(1)} %add_add_fusion.8), channel_id=1, source_target_pairs={{0,8},{1,9},{2,10},{3,11},{4,12},{5,13},{6,14},{7,15},{8,0},{9,1},... | collective-permute-start | bytes 1044488 | tf_op jit(solution)/shard_map/ppermute | solution.py:282
  39.3 11.4 %collective-permute-start.24 = (f32[688,128]{1,0:T(8,128)S(1)}, f32[688,128]{1,0:T(8,128)S(1)}, u32[]{:S(2)}, u32[]{:S(2)}) collective-permute-start(f32[688,128]{1,0:T(8,128)S(1)} %add_add_fusion.2), channel_id=1, source_target_pairs={{0,2},{1,3},{2,0},{3,1},{4,6},{5,7},{6,4},{7,5},{8,10},{9,11},{10,... | collective-permute-start | bytes 1056776 | tf_op jit(solution)/shard_map/ppermute | solution.py:282
  39.8 17.0 %collective-permute-start.11 = (f32[5,136,128]{2,1,0:T(8,128)S(1)}, f32[5,136,128]{2,1,0:T(8,128)S(1)}, u32[]{:S(2)}, u32[]{:S(2)}) collective-permute-start(f32[5,136,128]{2,1,0:T(8,128)S(1)} %multiply_add_fusion.21), channel_id=1, source_target_pairs={{0,9},{1,8},{2,11},{3,10},{4,13},{5,12},{6,15},{7,14},{8,1},{9,0},... | collective-permute-start | bytes 1044488 | tf_op jit(solution)/shard_map/ppermute | solution.py:282
  43.2 13.8 %collective-permute-start.18 = (f32[17,40,128]{2,1,0:T(8,128)S(1)}, f32[17,40,128]{2,1,0:T(8,128)S(1)}, u32[]{:S(2)}, u32[]{:S(2)}) collective-permute-start(f32[17,40,128]{2,1,0:T(8,128)S(1)} %multiply_add_fusion.17), channel_id=1, source_target_pairs={{0,6},{1,7},{2,4},{3,5},{4,2},{5,3},{6,0},{7,1},{8,14},{9,15},{10,... | collective-permute-start | bytes 1044488 | tf_op jit(solution)/shard_map/ppermute | solution.py:282
  44.6 14.2 %collective-permute-start.32 = (f32[680,128]{1,0:T(8,128)S(1)}, f32[680,128]{1,0:T(8,128)S(1)}, u32[]{:S(2)}, u32[]{:S(2)}) collective-permute-start(f32[680,128]{1,0:T(8,128)S(1)} %multiply_add_fusion.13), channel_id=1, source_target_pairs={{0,96},{1,97},{2,98},{3,99},{4,100},{5,101},{6,102},{7,103},{8,104... | collective-permute-start | bytes 1044488 | tf_op jit(solution)/shard_map/ppermute | solution.py:282
  48.6 10.3 %collective-permute-start.39 = (f32[85,8,128]{2,1,0:T(8,128)S(1)}, f32[85,8,128]{2,1,0:T(8,128)S(1)}, u32[]{:S(2)}, u32[]{:S(2)}) collective-permute-start(f32[85,8,128]{2,1,0:T(8,128)S(1)} %multiply_add_fusion.9), channel_id=1, source_target_pairs={{0,9},{1,8},{2,11},{3,10},{4,13},{5,12},{6,15},{7,14},{8,1},{9,0},... | collective-permute-start | bytes 1044488 | tf_op jit(solution)/shard_map/ppermute | solution.py:282
  50.7 15.1 %collective-permute-start.4 = (f32[43,16,128]{2,1,0:T(8,128)S(1)}, f32[43,16,128]{2,1,0:T(8,128)S(1)}, u32[]{:S(2)}, u32[]{:S(2)}) collective-permute-start(f32[43,16,128]{2,1,0:T(8,128)S(1)} %multiply_add_fusion.5), channel_id=1, source_target_pairs={{0,96},{1,97},{2,98},{3,99},{4,100},{5,101},{6,102},{7,103},{8,104... | collective-permute-start | bytes 1056776 | tf_op jit(solution)/shard_map/ppermute | solution.py:282
  56.8 12.3 %collective-permute-start.25 = (f32[688,128]{1,0:T(8,128)S(1)}, f32[688,128]{1,0:T(8,128)S(1)}, u32[]{:S(2)}, u32[]{:S(2)}) collective-permute-start(f32[688,128]{1,0:T(8,128)S(1)} %multiply_add_fusion.1), channel_id=1, source_target_pairs={{0,6},{1,7},{2,4},{3,5},{4,2},{5,3},{6,0},{7,1},{8,14},{9,15},{10,... | collective-permute-start | bytes 1056776 | tf_op jit(solution)/shard_map/ppermute | solution.py:282
  57.0 12.2 %collective-permute-start.12 = (f32[5,136,128]{2,1,0:T(8,128)S(1)}, f32[5,136,128]{2,1,0:T(8,128)S(1)}, u32[]{:S(2)}, u32[]{:S(2)}) collective-permute-start(f32[5,136,128]{2,1,0:T(8,128)S(1)} %add_add_fusion.16), channel_id=1, source_target_pairs={{0,2},{1,3},{2,0},{3,1},{4,6},{5,7},{6,4},{7,5},{8,10},{9,11},{10,... | collective-permute-start | bytes 1044488 | tf_op jit(solution)/shard_map/ppermute | solution.py:282
  58.7 10.6 %collective-permute-start.19 = (f32[17,40,128]{2,1,0:T(8,128)S(1)}, f32[17,40,128]{2,1,0:T(8,128)S(1)}, u32[]{:S(2)}, u32[]{:S(2)}) collective-permute-start(f32[17,40,128]{2,1,0:T(8,128)S(1)} %add_add_fusion.13), channel_id=1, source_target_pairs={{0,32},{1,33},{2,34},{3,35},{4,36},{5,37},{6,38},{7,39},{8,40},{9,... | collective-permute-start | bytes 1044488 | tf_op jit(solution)/shard_map/ppermute | solution.py:282
  58.9 12.1 %collective-permute-start.33 = (f32[680,128]{1,0:T(8,128)S(1)}, f32[680,128]{1,0:T(8,128)S(1)}, u32[]{:S(2)}, u32[]{:S(2)}) collective-permute-start(f32[680,128]{1,0:T(8,128)S(1)} %add_add_fusion.10), channel_id=1, source_target_pairs={{0,8},{1,9},{2,10},{3,11},{4,12},{5,13},{6,14},{7,15},{8,0},{9,1},... | collective-permute-start | bytes 1044488 | tf_op jit(solution)/shard_map/ppermute | solution.py:282
  65.8 11.0 %collective-permute-start.40 = (f32[85,8,128]{2,1,0:T(8,128)S(1)}, f32[85,8,128]{2,1,0:T(8,128)S(1)}, u32[]{:S(2)}, u32[]{:S(2)}) collective-permute-start(f32[85,8,128]{2,1,0:T(8,128)S(1)} %add_add_fusion.7), channel_id=1, source_target_pairs={{0,2},{1,3},{2,0},{3,1},{4,6},{5,7},{6,4},{7,5},{8,10},{9,11},{10,... | collective-permute-start | bytes 1044488 | tf_op jit(solution)/shard_map/ppermute | solution.py:282
  69.1 11.1 %collective-permute-start.5 = (f32[43,16,128]{2,1,0:T(8,128)S(1)}, f32[43,16,128]{2,1,0:T(8,128)S(1)}, u32[]{:S(2)}, u32[]{:S(2)}) collective-permute-start(f32[43,16,128]{2,1,0:T(8,128)S(1)} %add_add_fusion.4), channel_id=1, source_target_pairs={{0,8},{1,9},{2,10},{3,11},{4,12},{5,13},{6,14},{7,15},{8,0},{9,1},... | collective-permute-start | bytes 1056776 | tf_op jit(solution)/shard_map/ppermute | solution.py:282
  69.2 11.0 %collective-permute-start.26 = (f32[688,128]{1,0:T(8,128)S(1)}, f32[688,128]{1,0:T(8,128)S(1)}, u32[]{:S(2)}, u32[]{:S(2)}) collective-permute-start(f32[688,128]{1,0:T(8,128)S(1)} %add_add_fusion.1), channel_id=1, source_target_pairs={{0,32},{1,33},{2,34},{3,35},{4,36},{5,37},{6,38},{7,39},{8,40},{9,... | collective-permute-start | bytes 1056776 | tf_op jit(solution)/shard_map/ppermute | solution.py:282
  69.4 12.2 %collective-permute-start.13 = (f32[5,136,128]{2,1,0:T(8,128)S(1)}, f32[5,136,128]{2,1,0:T(8,128)S(1)}, u32[]{:S(2)}, u32[]{:S(2)}) collective-permute-start(f32[5,136,128]{2,1,0:T(8,128)S(1)} %multiply_add_fusion.20), channel_id=1, source_target_pairs={{0,6},{1,7},{2,4},{3,5},{4,2},{5,3},{6,0},{7,1},{8,14},{9,15},{10,... | collective-permute-start | bytes 1044488 | tf_op jit(solution)/shard_map/ppermute | solution.py:282
  71.0 15.1 %collective-permute-start.20 = (f32[17,40,128]{2,1,0:T(8,128)S(1)}, f32[17,40,128]{2,1,0:T(8,128)S(1)}, u32[]{:S(2)}, u32[]{:S(2)}) collective-permute-start(f32[17,40,128]{2,1,0:T(8,128)S(1)} %multiply_add_fusion.16), channel_id=1, source_target_pairs={{0,96},{1,97},{2,98},{3,99},{4,100},{5,101},{6,102},{7,103},{8,104... | collective-permute-start | bytes 1044488 | tf_op jit(solution)/shard_map/ppermute | solution.py:282
  80.2 13.3 %collective-permute-start.6 = (f32[43,16,128]{2,1,0:T(8,128)S(1)}, f32[43,16,128]{2,1,0:T(8,128)S(1)}, u32[]{:S(2)}, u32[]{:S(2)}) collective-permute-start(f32[43,16,128]{2,1,0:T(8,128)S(1)} %multiply_add_fusion.4), channel_id=1, source_target_pairs={{0,9},{1,8},{2,11},{3,10},{4,13},{5,12},{6,15},{7,14},{8,1},{9,0},... | collective-permute-start | bytes 1056776 | tf_op jit(solution)/shard_map/ppermute | solution.py:282
  (18 other events, 132.4 us)

commit v4 on v3

--- a/solution.py
+++ b/solution.py
@@ -99,7 +99,11 @@
 def phase_kernel(x_hbm, j_ref, f_ref, *refs):
     outs, (coef_ref, tan_ref, x_ref, sems) = refs[:COUNT], refs[COUNT:]
     copies = [
-        pltpu.make_async_copy(x_hbm.at[pl.ds(1024 * h, 1024), :], x_ref.at[pl.ds(1024 * h, 1024), :], sems.at[h])
+        pltpu.make_async_copy(
+            x_hbm.at[pl.ds(32 * h, 32), :, :],
+            x_ref.reshape(128, 40, 128).at[pl.ds(32 * h, 32), pl.ds(0, 32), :],
+            sems.at[h],
+        )
         for h in range(4)
     ]
     for copy in copies:
@@ -165,8 +169,8 @@
             copies[at // 32].wait()
         values = [[], []]
         for rl in range(16):
-            xre = x_ref[pl.ds(at * 32 + 2 * rl, 8, stride=32), :]
-            xim = x_ref[pl.ds(at * 32 + 2 * rl + 1, 8, stride=32), :]
+            xre = x_ref[pl.ds(at * 40 + 2 * rl, 8, stride=40), :]
+            xim = x_ref[pl.ds(at * 40 + 2 * rl + 1, 8, stride=40), :]
             er, ei = e1r[rl : rl + 1, :], e1i[rl : rl + 1, :]
             cr, ci = (c[at : at + 8, :] for c in columns[rl >> 3])
             yre, yim = xre * er - xim * ei, xre * ei + xim * er
@@ -193,7 +197,7 @@
     rows = lax.broadcasted_iota(jnp.int32, (128, 128), 0)
     cols = lax.broadcasted_iota(jnp.int32, (128, 128), 1)
     turns = ones_in(rows, 7) + ones_in(cols, 7) + device_ones
-    width = 2 * (last - first)
+    width = 2 * (last - first) + 8
 
     def read(row):
         parts = []
@@ -256,7 +260,7 @@
 
 
 def shards(amplitudes, couplings, fields):
-    rows = amplitudes.reshape(2, 2048, 128).transpose(1, 0, 2).reshape(4096, 128)
+    rows = amplitudes.reshape(2, 2048, 128).transpose(1, 0, 2).reshape(128, 32, 128)
     vmem = pl.BlockSpec(memory_space=pltpu.VMEM)
     smem = pl.BlockSpec(memory_space=pltpu.SMEM)
     hbm = pl.BlockSpec(memory_space=pl.ANY)
@@ -266,7 +270,7 @@
         + [pltpu.VMEM((16, 128), F32), pltpu.VMEM((32, 128), F32)],
         in_specs=[hbm, smem, smem],
         out_specs=[vmem] * (COUNT + 2),
-        scratch_shapes=[pltpu.VMEM((4096, 128), F32), pltpu.SemaphoreType.DMA((4,))],
+        scratch_shapes=[pltpu.VMEM((5120, 128), F32), pltpu.SemaphoreType.DMA((4,))],
         name="phase_step",
     )(rows, couplings, fields)
     streams, (coef, tangents) = list(made[:COUNT]), made[COUNT:]
@@ -291,7 +295,7 @@
         return pltpu.with_memory_space_constraint(value, pltpu.VMEM)
 
     out_shape = jax.ShapeDtypeStruct((128, 32, 128), F32)
-    scratch = [pltpu.VMEM((2048, 128), F32), pltpu.SemaphoreType.DMA((2,))]
+    scratch = [pltpu.VMEM((3072, 128), F32), pltpu.SemaphoreType.DMA((2,))]
     params = pltpu.CompilerParams(vmem_limit_bytes=8 << 20)
     out, lane_mat, high_mat = pl.pallas_call(
         first_final_kernel,

time: 97.4 us -> 96.5 us (level)
  the two profiles are of different devices: /device:TPU:0 before, /device:TPU:16 now
where the time goes in v4:
time: 96.5 us; the launch traced here: 96.3 us
  starting transfers between devices  63.5 us (66%)
  waiting for transfers between devices  23 us (24%)
  Pallas kernels  6.8 us (7%)
  other arithmetic  2.51 us (3%)
    ppermute x36, starting transfers between devices, shards(): got = lax.ppermute(streams[i], AXES, pairs_of('xyz'[k], first))  62.2 us
    ppermute x36, waiting for transfers between devices, shards(): got = lax.ppermute(streams[i], AXES, pairs_of('xyz'[k], first))  22.1 us
    pallas_call x1, Pallas kernels, shards(): pl.pallas_call(phase_kernel, out_shape=[pltpu.VMEM(s, F32) for s in SHAPE...  3.06 us
    pallas_call x1, Pallas kernels, shards(): pl.pallas_call(first_final_kernel, out_shape=[out_shape, pltpu.VMEM((256,...  1.96 us
  transfers between devices with their start and end apart: 42, of which 15 were waited for; matrix products, arithmetic and copies ran while one was open for 3% of the time, Pallas kernels for 2%

profile of v4, /device:TPU:16, one launch (start us, length us, event | category | flops | bytes accessed | tf_op | source)
XLA Modules:
  0.0 96.3 jit_solution(13148445784264319757)
XLA Ops:
  0.0 3.1 %phase_step.1 = (f32[688,128]{1,0:T(8,128)S(1)}, f32[680,128]{1,0:T(8,128)S(1)}, f32[85,8,128]{2,1,0:T(8,128)S(1)}, f32[43,16,128]{2,1,0:T(8,128)S(1)}, f32[5,13...) custom-call(f32[128,32,128]{2,1,0:T(8,128)} %bitcast.30, ...), custom_call_target="tpu_custom_call" | custom-call | tf_op jit(solution)/shard_map/phase_step/pallas_call | solution.py:267
  5.3 1.9 %collective-permute-start.8 = (f32[5,136,128]{2,1,0:T(8,128)S(1)}, f32[5,136,128]{2,1,0:T(8,128)S(1)}, u32[]{:S(2)}, u32[]{:S(2)}) collective-permute-start(f32[5,136,128]{2,1,0:T(8,128)S(1)} %multiply_add_fusion.23), channel_id=1, source_target_pairs={{0,32},{1,33},{2,34},{3,35},{4,36},{5,37},{6,38},{7,39},{8,40},{9,... | collective-permute-start | bytes 1044488 | tf_op jit(solution)/shard_map/ppermute | solution.py:286
  7.3 1.6 %collective-permute-start.15 = (f32[17,40,128]{2,1,0:T(8,128)S(1)}, f32[17,40,128]{2,1,0:T(8,128)S(1)}, u32[]{:S(2)}, u32[]{:S(2)}) collective-permute-start(f32[17,40,128]{2,1,0:T(8,128)S(1)} %multiply_add_fusion.19), channel_id=1, source_target_pairs={{0,8},{1,9},{2,10},{3,11},{4,12},{5,13},{6,14},{7,15},{8,0},{9,1},... | collective-permute-start | bytes 1044488 | tf_op jit(solution)/shard_map/ppermute | solution.py:286
  14.7 3.6 %collective-permute-start.9 = (f32[5,136,128]{2,1,0:T(8,128)S(1)}, f32[5,136,128]{2,1,0:T(8,128)S(1)}, u32[]{:S(2)}, u32[]{:S(2)}) collective-permute-start(f32[5,136,128]{2,1,0:T(8,128)S(1)} %multiply_add_fusion.22), channel_id=1, source_target_pairs={{0,96},{1,97},{2,98},{3,99},{4,100},{5,101},{6,102},{7,103},{8,104... | collective-permute-start | bytes 1044488 | tf_op jit(solution)/shard_map/ppermute | solution.py:286
  18.3 2.2 %collective-permute-start.16 = (f32[17,40,128]{2,1,0:T(8,128)S(1)}, f32[17,40,128]{2,1,0:T(8,128)S(1)}, u32[]{:S(2)}, u32[]{:S(2)}) collective-permute-start(f32[17,40,128]{2,1,0:T(8,128)S(1)} %multiply_add_fusion.18), channel_id=1, source_target_pairs={{0,9},{1,8},{2,11},{3,10},{4,13},{5,12},{6,15},{7,14},{8,1},{9,0},... | collective-permute-start | bytes 1044488 | tf_op jit(solution)/shard_map/ppermute | solution.py:286
  23.6 2.4 %collective-permute-start.23 = (f32[688,128]{1,0:T(8,128)S(1)}, f32[688,128]{1,0:T(8,128)S(1)}, u32[]{:S(2)}, u32[]{:S(2)}) collective-permute-start(f32[688,128]{1,0:T(8,128)S(1)} %multiply_add_fusion.2), channel_id=1, source_target_pairs={{0,9},{1,8},{2,11},{3,10},{4,13},{5,12},{6,15},{7,14},{8,1},{9,0},... | collective-permute-start | bytes 1056776 | tf_op jit(solution)/shard_map/ppermute | solution.py:286
  27.9 2.5 %collective-permute-start.17 = (f32[17,40,128]{2,1,0:T(8,128)S(1)}, f32[17,40,128]{2,1,0:T(8,128)S(1)}, u32[]{:S(2)}, u32[]{:S(2)}) collective-permute-start(f32[17,40,128]{2,1,0:T(8,128)S(1)} %add_add_fusion.14), channel_id=1, source_target_pairs={{0,2},{1,3},{2,0},{3,1},{4,6},{5,7},{6,4},{7,5},{8,10},{9,11},{10,... | collective-permute-start | bytes 1044488 | tf_op jit(solution)/shard_map/ppermute | solution.py:286
  31.9 1.9 %collective-permute-start.38 = (f32[85,8,128]{2,1,0:T(8,128)S(1)}, f32[85,8,128]{2,1,0:T(8,128)S(1)}, u32[]{:S(2)}, u32[]{:S(2)}) collective-permute-start(f32[85,8,128]{2,1,0:T(8,128)S(1)} %add_add_fusion.8), channel_id=1, source_target_pairs={{0,8},{1,9},{2,10},{3,11},{4,12},{5,13},{6,14},{7,15},{8,0},{9,1},... | collective-permute-start | bytes 1044488 | tf_op jit(solution)/shard_map/ppermute | solution.py:286
  33.8 1.8 %collective-permute-done.23 = f32[688,128]{1,0:T(8,128)S(1)} collective-permute-done((f32[688,128]{1,0:T(8,128)S(1)}, f32[688,128]{1,0:T(8,128)S(1)}, u32[]{:S(2)}, u32[]{:S(2)}) %collective-permute-start.23) | collective-permute-done | bytes 352288 | tf_op jit(solution)/shard_map/ppermute | solution.py:286
  35.9 3.6 %collective-permute-start.24 = (f32[688,128]{1,0:T(8,128)S(1)}, f32[688,128]{1,0:T(8,128)S(1)}, u32[]{:S(2)}, u32[]{:S(2)}) collective-permute-start(f32[688,128]{1,0:T(8,128)S(1)} %add_add_fusion.2), channel_id=1, source_target_pairs={{0,2},{1,3},{2,0},{3,1},{4,6},{5,7},{6,4},{7,5},{8,10},{9,11},{10,... | collective-permute-start | bytes 1056776 | tf_op jit(solution)/shard_map/ppermute | solution.py:286
  40.7 2.4 %collective-permute-start.18 = (f32[17,40,128]{2,1,0:T(8,128)S(1)}, f32[17,40,128]{2,1,0:T(8,128)S(1)}, u32[]{:S(2)}, u32[]{:S(2)}) collective-permute-start(f32[17,40,128]{2,1,0:T(8,128)S(1)} %multiply_add_fusion.17), channel_id=1, source_target_pairs={{0,6},{1,7},{2,4},{3,5},{4,2},{5,3},{6,0},{7,1},{8,14},{9,15},{10,... | collective-permute-start | bytes 1044488 | tf_op jit(solution)/shard_map/ppermute | solution.py:286
  43.2 2.9 %collective-permute-start.32 = (f32[680,128]{1,0:T(8,128)S(1)}, f32[680,128]{1,0:T(8,128)S(1)}, u32[]{:S(2)}, u32[]{:S(2)}) collective-permute-start(f32[680,128]{1,0:T(8,128)S(1)} %multiply_add_fusion.13), channel_id=1, source_target_pairs={{0,96},{1,97},{2,98},{3,99},{4,100},{5,101},{6,102},{7,103},{8,104... | collective-permute-start | bytes 1044488 | tf_op jit(solution)/shard_map/ppermute | solution.py:286
  46.2 4.5 %collective-permute-start.39 = (f32[85,8,128]{2,1,0:T(8,128)S(1)}, f32[85,8,128]{2,1,0:T(8,128)S(1)}, u32[]{:S(2)}, u32[]{:S(2)}) collective-permute-start(f32[85,8,128]{2,1,0:T(8,128)S(1)} %multiply_add_fusion.9), channel_id=1, source_target_pairs={{0,9},{1,8},{2,11},{3,10},{4,13},{5,12},{6,15},{7,14},{8,1},{9,0},... | collective-permute-start | bytes 1044488 | tf_op jit(solution)/shard_map/ppermute | solution.py:286
  50.8 2.7 %collective-permute-start.4 = (f32[43,16,128]{2,1,0:T(8,128)S(1)}, f32[43,16,128]{2,1,0:T(8,128)S(1)}, u32[]{:S(2)}, u32[]{:S(2)}) collective-permute-start(f32[43,16,128]{2,1,0:T(8,128)S(1)} %multiply_add_fusion.5), channel_id=1, source_target_pairs={{0,96},{1,97},{2,98},{3,99},{4,100},{5,101},{6,102},{7,103},{8,104... | collective-permute-start | bytes 1056776 | tf_op jit(solution)/shard_map/ppermute | solution.py:286
  53.6 2.7 %collective-permute-start.25 = (f32[688,128]{1,0:T(8,128)S(1)}, f32[688,128]{1,0:T(8,128)S(1)}, u32[]{:S(2)}, u32[]{:S(2)}) collective-permute-start(f32[688,128]{1,0:T(8,128)S(1)} %multiply_add_fusion.1), channel_id=1, source_target_pairs={{0,6},{1,7},{2,4},{3,5},{4,2},{5,3},{6,0},{7,1},{8,14},{9,15},{10,... | collective-permute-start | bytes 1056776 | tf_op jit(solution)/shard_map/ppermute | solution.py:286
  58.4 2.9 %collective-permute-done.4 = f32[43,16,128]{2,1,0:T(8,128)S(1)} collective-permute-done((f32[43,16,128]{2,1,0:T(8,128)S(1)}, f32[43,16,128]{2,1,0:T(8,128)S(1)}, u32[]{:S(2)}, u32[]{:S(2)}) %collective-permute-start.4) | collective-permute-done | bytes 352288 | tf_op jit(solution)/shard_map/ppermute | solution.py:286
  62.5 1.8 %collective-permute-done.25 = f32[688,128]{1,0:T(8,128)S(1)} collective-permute-done((f32[688,128]{1,0:T(8,128)S(1)}, f32[688,128]{1,0:T(8,128)S(1)}, u32[]{:S(2)}, u32[]{:S(2)}) %collective-permute-start.25) | collective-permute-done | bytes 352288 | tf_op jit(solution)/shard_map/ppermute | solution.py:286
  68.0 5.0 %collective-permute-done.40 = f32[85,8,128]{2,1,0:T(8,128)S(1)} collective-permute-done((f32[85,8,128]{2,1,0:T(8,128)S(1)}, f32[85,8,128]{2,1,0:T(8,128)S(1)}, u32[]{:S(2)}, u32[]{:S(2)}) %collective-permute-start.40) | collective-permute-done | bytes 348192 | tf_op jit(solution)/shard_map/ppermute | solution.py:286
  73.0 2.0 %collective-permute-start.34 = (f32[680,128]{1,0:T(8,128)S(1)}, f32[680,128]{1,0:T(8,128)S(1)}, u32[]{:S(2)}, u32[]{:S(2)}) collective-permute-start(f32[680,128]{1,0:T(8,128)S(1)} %multiply_add_fusion.12), channel_id=1, source_target_pairs={{0,9},{1,8},{2,11},{3,10},{4,13},{5,12},{6,15},{7,14},{8,1},{9,0},... | collective-permute-start | bytes 1044488 | tf_op jit(solution)/shard_map/ppermute | solution.py:286
  75.4 4.2 %collective-permute-start.41 = (f32[85,8,128]{2,1,0:T(8,128)S(1)}, f32[85,8,128]{2,1,0:T(8,128)S(1)}, u32[]{:S(2)}, u32[]{:S(2)}) collective-permute-start(f32[85,8,128]{2,1,0:T(8,128)S(1)} %multiply_add_fusion.8), channel_id=1, source_target_pairs={{0,6},{1,7},{2,4},{3,5},{4,2},{5,3},{6,0},{7,1},{8,14},{9,15},{10,... | collective-permute-start | bytes 1044488 | tf_op jit(solution)/shard_map/ppermute | solution.py:286
  79.8 7.1 %collective-permute-start.27 = (f32[688,128]{1,0:T(8,128)S(1)}, f32[688,128]{1,0:T(8,128)S(1)}, u32[]{:S(2)}, u32[]{:S(2)}) collective-permute-start(f32[688,128]{1,0:T(8,128)S(1)} %multiply_add_fusion), channel_id=1, source_target_pairs={{0,96},{1,97},{2,98},{3,99},{4,100},{5,101},{6,102},{7,103},{8,104... | collective-permute-start | bytes 1056776 | tf_op jit(solution)/shard_map/ppermute | solution.py:286
  87.3 5.0 %collective-permute-done.27 = f32[688,128]{1,0:T(8,128)S(1)} collective-permute-done((f32[688,128]{1,0:T(8,128)S(1)}, f32[688,128]{1,0:T(8,128)S(1)}, u32[]{:S(2)}, u32[]{:S(2)}) %collective-permute-start.27) | collective-permute-done | bytes 352288 | tf_op jit(solution)/shard_map/ppermute | solution.py:286
  92.3 2.0 %first_final.1 = (f32[128,32,128]{2,1,0:T(8,128)}, bf16[256,256]{1,0:T(8,128)(2,1)S(1)}, bf16[128,384]{1,0:T(8,128)(2,1)S(1)}) custom-call(f32[688,128]{1,0:T(8,128)S(1)} %add_add_fusion.refs_0_, f32[680,128]{1,0:T(8,128)S(1)} %add_add_fusion.9.refs_1_, f32[85,8,128]{2,1,0:T(8,128)S(1)} %add_add_fusion.6.refs_2_, f32[32,128]{1,0:T(8,128)S(1)} %get-tuple-element.23.refs_3_), custom_call_target="tpu_custom_call" | custom-call | tf_op jit(solution)/shard_map/first_final/pallas_call | solution.py:300
  94.4 1.8 %second_final.1 = f32[128,32,128]{2,1,0:T(8,128)} custom-call(f32[43,16,128]{2,1,0:T(8,128)S(1)} %add_add_fusion.3.refs_0_, f32[5,136,128]{2,1,0:T(8,128)S(1)} %add_add_fusion.15.refs_1_, f32[17,40,128]{2,1,0:T(8,128)S(1)} %add_add_fusion.12.refs_2_, bf16[256,256]{1,0:T(8,128)(2,1)S(1)} %get-tuple-element.24.refs_3_, ...), custom_call_target="tpu_custom_call", output_to_operand_aliasing={{}: (5, {})} | custom-call | tf_op jit(solution)/shard_map/second_final/pallas_call | solution.py:309
  (106 shorter events, 24.3 us)
Async XLA Ops:
  10.4 10.2 %collective-permute-start.36 = (f32[85,8,128]{2,1,0:T(8,128)S(1)}, f32[85,8,128]{2,1,0:T(8,128)S(1)}, u32[]{:S(2)}, u32[]{:S(2)}) collective-permute-start(f32[85,8,128]{2,1,0:T(8,128)S(1)} %multiply_add_fusion.11), channel_id=1, source_target_pairs={{0,32},{1,33},{2,34},{3,35},{4,36},{5,37},{6,38},{7,39},{8,40},{9,... | collective-permute-start | bytes 1044488 | tf_op jit(solution)/shard_map/ppermute | solution.py:286
  10.8 10.3 %collective-permute-start.1 = (f32[43,16,128]{2,1,0:T(8,128)S(1)}, f32[43,16,128]{2,1,0:T(8,128)S(1)}, u32[]{:S(2)}, u32[]{:S(2)}) collective-permute-start(f32[43,16,128]{2,1,0:T(8,128)S(1)} %multiply_add_fusion.7), channel_id=1, source_target_pairs={{0,2},{1,3},{2,0},{3,1},{4,6},{5,7},{6,4},{7,5},{8,10},{9,11},{10,... | collective-permute-start | bytes 1056776 | tf_op jit(solution)/shard_map/ppermute | solution.py:286
  12.6 10.1 %collective-permute-start.22 = (f32[688,128]{1,0:T(8,128)S(1)}, f32[688,128]{1,0:T(8,128)S(1)}, u32[]{:S(2)}, u32[]{:S(2)}) collective-permute-start(f32[688,128]{1,0:T(8,128)S(1)} %multiply_add_fusion.3), channel_id=1, source_target_pairs={{0,8},{1,9},{2,10},{3,11},{4,12},{5,13},{6,14},{7,15},{8,0},{9,1},... | collective-permute-start | bytes 1056776 | tf_op jit(solution)/shard_map/ppermute | solution.py:286
  23.6 12.0 %collective-permute-start.23 = (f32[688,128]{1,0:T(8,128)S(1)}, f32[688,128]{1,0:T(8,128)S(1)}, u32[]{:S(2)}, u32[]{:S(2)}) collective-permute-start(f32[688,128]{1,0:T(8,128)S(1)} %multiply_add_fusion.2), channel_id=1, source_target_pairs={{0,9},{1,8},{2,11},{3,10},{4,13},{5,12},{6,15},{7,14},{8,1},{9,0},... | collective-permute-start | bytes 1056776 | tf_op jit(solution)/shard_map/ppermute | solution.py:286
  27.9 11.6 %collective-permute-start.17 = (f32[17,40,128]{2,1,0:T(8,128)S(1)}, f32[17,40,128]{2,1,0:T(8,128)S(1)}, u32[]{:S(2)}, u32[]{:S(2)}) collective-permute-start(f32[17,40,128]{2,1,0:T(8,128)S(1)} %add_add_fusion.14), channel_id=1, source_target_pairs={{0,2},{1,3},{2,0},{3,1},{4,6},{5,7},{6,4},{7,5},{8,10},{9,11},{10,... | collective-permute-start | bytes 1044488 | tf_op jit(solution)/shard_map/ppermute | solution.py:286
  30.5 10.2 %collective-permute-start.31 = (f32[680,128]{1,0:T(8,128)S(1)}, f32[680,128]{1,0:T(8,128)S(1)}, u32[]{:S(2)}, u32[]{:S(2)}) collective-permute-start(f32[680,128]{1,0:T(8,128)S(1)} %add_add_fusion.11), channel_id=1, source_target_pairs={{0,32},{1,33},{2,34},{3,35},{4,36},{5,37},{6,38},{7,39},{8,40},{9,... | collective-permute-start | bytes 1044488 | tf_op jit(solution)/shard_map/ppermute | solution.py:286
  31.9 11.4 %collective-permute-start.38 = (f32[85,8,128]{2,1,0:T(8,128)S(1)}, f32[85,8,128]{2,1,0:T(8,128)S(1)}, u32[]{:S(2)}, u32[]{:S(2)}) collective-permute-start(f32[85,8,128]{2,1,0:T(8,128)S(1)} %add_add_fusion.8), channel_id=1, source_target_pairs={{0,8},{1,9},{2,10},{3,11},{4,12},{5,13},{6,14},{7,15},{8,0},{9,1},... | collective-permute-start | bytes 1044488 | tf_op jit(solution)/shard_map/ppermute | solution.py:286
  35.6 10.6 %collective-permute-start.3 = (f32[43,16,128]{2,1,0:T(8,128)S(1)}, f32[43,16,128]{2,1,0:T(8,128)S(1)}, u32[]{:S(2)}, u32[]{:S(2)}) collective-permute-start(f32[43,16,128]{2,1,0:T(8,128)S(1)} %add_add_fusion.5), channel_id=1, source_target_pairs={{0,32},{1,33},{2,34},{3,35},{4,36},{5,37},{6,38},{7,39},{8,40},{9,... | collective-permute-start | bytes 1056776 | tf_op jit(solution)/shard_map/ppermute | solution.py:286
  35.9 14.9 %collective-permute-start.24 = (f32[688,128]{1,0:T(8,128)S(1)}, f32[688,128]{1,0:T(8,128)S(1)}, u32[]{:S(2)}, u32[]{:S(2)}) collective-permute-start(f32[688,128]{1,0:T(8,128)S(1)} %add_add_fusion.2), channel_id=1, source_target_pairs={{0,2},{1,3},{2,0},{3,1},{4,6},{5,7},{6,4},{7,5},{8,10},{9,11},{10,... | collective-permute-start | bytes 1056776 | tf_op jit(solution)/shard_map/ppermute | solution.py:286
  39.5 14.0 %collective-permute-start.11 = (f32[5,136,128]{2,1,0:T(8,128)S(1)}, f32[5,136,128]{2,1,0:T(8,128)S(1)}, u32[]{:S(2)}, u32[]{:S(2)}) collective-permute-start(f32[5,136,128]{2,1,0:T(8,128)S(1)} %multiply_add_fusion.21), channel_id=1, source_target_pairs={{0,9},{1,8},{2,11},{3,10},{4,13},{5,12},{6,15},{7,14},{8,1},{9,0},... | collective-permute-start | bytes 1044488 | tf_op jit(solution)/shard_map/ppermute | solution.py:286
  40.7 15.7 %collective-permute-start.18 = (f32[17,40,128]{2,1,0:T(8,128)S(1)}, f32[17,40,128]{2,1,0:T(8,128)S(1)}, u32[]{:S(2)}, u32[]{:S(2)}) collective-permute-start(f32[17,40,128]{2,1,0:T(8,128)S(1)} %multiply_add_fusion.17), channel_id=1, source_target_pairs={{0,6},{1,7},{2,4},{3,5},{4,2},{5,3},{6,0},{7,1},{8,14},{9,15},{10,... | collective-permute-start | bytes 1044488 | tf_op jit(solution)/shard_map/ppermute | solution.py:286
  43.2 14.6 %collective-permute-start.32 = (f32[680,128]{1,0:T(8,128)S(1)}, f32[680,128]{1,0:T(8,128)S(1)}, u32[]{:S(2)}, u32[]{:S(2)}) collective-permute-start(f32[680,128]{1,0:T(8,128)S(1)} %multiply_add_fusion.13), channel_id=1, source_target_pairs={{0,96},{1,97},{2,98},{3,99},{4,100},{5,101},{6,102},{7,103},{8,104... | collective-permute-start | bytes 1044488 | tf_op jit(solution)/shard_map/ppermute | solution.py:286
  46.2 11.8 %collective-permute-start.39 = (f32[85,8,128]{2,1,0:T(8,128)S(1)}, f32[85,8,128]{2,1,0:T(8,128)S(1)}, u32[]{:S(2)}, u32[]{:S(2)}) collective-permute-start(f32[85,8,128]{2,1,0:T(8,128)S(1)} %multiply_add_fusion.9), channel_id=1, source_target_pairs={{0,9},{1,8},{2,11},{3,10},{4,13},{5,12},{6,15},{7,14},{8,1},{9,0},... | collective-permute-start | bytes 1044488 | tf_op jit(solution)/shard_map/ppermute | solution.py:286
  50.8 10.5 %collective-permute-start.4 = (f32[43,16,128]{2,1,0:T(8,128)S(1)}, f32[43,16,128]{2,1,0:T(8,128)S(1)}, u32[]{:S(2)}, u32[]{:S(2)}) collective-permute-start(f32[43,16,128]{2,1,0:T(8,128)S(1)} %multiply_add_fusion.5), channel_id=1, source_target_pairs={{0,96},{1,97},{2,98},{3,99},{4,100},{5,101},{6,102},{7,103},{8,104... | collective-permute-start | bytes 1056776 | tf_op jit(solution)/shard_map/ppermute | solution.py:286
  53.6 10.7 %collective-permute-start.25 = (f32[688,128]{1,0:T(8,128)S(1)}, f32[688,128]{1,0:T(8,128)S(1)}, u32[]{:S(2)}, u32[]{:S(2)}) collective-permute-start(f32[688,128]{1,0:T(8,128)S(1)} %multiply_add_fusion.1), channel_id=1, source_target_pairs={{0,6},{1,7},{2,4},{3,5},{4,2},{5,3},{6,0},{7,1},{8,14},{9,15},{10,... | collective-permute-start | bytes 1056776 | tf_op jit(solution)/shard_map/ppermute | solution.py:286
  61.3 11.7 %collective-permute-start.40 = (f32[85,8,128]{2,1,0:T(8,128)S(1)}, f32[85,8,128]{2,1,0:T(8,128)S(1)}, u32[]{:S(2)}, u32[]{:S(2)}) collective-permute-start(f32[85,8,128]{2,1,0:T(8,128)S(1)} %add_add_fusion.7), channel_id=1, source_target_pairs={{0,2},{1,3},{2,0},{3,1},{4,6},{5,7},{6,4},{7,5},{8,10},{9,11},{10,... | collective-permute-start | bytes 1044488 | tf_op jit(solution)/shard_map/ppermute | solution.py:286
  64.3 11.1 %collective-permute-start.5 = (f32[43,16,128]{2,1,0:T(8,128)S(1)}, f32[43,16,128]{2,1,0:T(8,128)S(1)}, u32[]{:S(2)}, u32[]{:S(2)}) collective-permute-start(f32[43,16,128]{2,1,0:T(8,128)S(1)} %add_add_fusion.4), channel_id=1, source_target_pairs={{0,8},{1,9},{2,10},{3,11},{4,12},{5,13},{6,14},{7,15},{8,0},{9,1},... | collective-permute-start | bytes 1056776 | tf_op jit(solution)/shard_map/ppermute | solution.py:286
  65.5 14.1 %collective-permute-start.26 = (f32[688,128]{1,0:T(8,128)S(1)}, f32[688,128]{1,0:T(8,128)S(1)}, u32[]{:S(2)}, u32[]{:S(2)}) collective-permute-start(f32[688,128]{1,0:T(8,128)S(1)} %add_add_fusion.1), channel_id=1, source_target_pairs={{0,32},{1,33},{2,34},{3,35},{4,36},{5,37},{6,38},{7,39},{8,40},{9,... | collective-permute-start | bytes 1056776 | tf_op jit(solution)/shard_map/ppermute | solution.py:286
  67.0 12.8 %collective-permute-start.13 = (f32[5,136,128]{2,1,0:T(8,128)S(1)}, f32[5,136,128]{2,1,0:T(8,128)S(1)}, u32[]{:S(2)}, u32[]{:S(2)}) collective-permute-start(f32[5,136,128]{2,1,0:T(8,128)S(1)} %multiply_add_fusion.20), channel_id=1, source_target_pairs={{0,6},{1,7},{2,4},{3,5},{4,2},{5,3},{6,0},{7,1},{8,14},{9,15},{10,... | collective-permute-start | bytes 1044488 | tf_op jit(solution)/shard_map/ppermute | solution.py:286
  67.1 20.0 %collective-permute-start.20 = (f32[17,40,128]{2,1,0:T(8,128)S(1)}, f32[17,40,128]{2,1,0:T(8,128)S(1)}, u32[]{:S(2)}, u32[]{:S(2)}) collective-permute-start(f32[17,40,128]{2,1,0:T(8,128)S(1)} %multiply_add_fusion.16), channel_id=1, source_target_pairs={{0,96},{1,97},{2,98},{3,99},{4,100},{5,101},{6,102},{7,103},{8,104... | collective-permute-start | bytes 1044488 | tf_op jit(solution)/shard_map/ppermute | solution.py:286
  73.0 14.1 %collective-permute-start.34 = (f32[680,128]{1,0:T(8,128)S(1)}, f32[680,128]{1,0:T(8,128)S(1)}, u32[]{:S(2)}, u32[]{:S(2)}) collective-permute-start(f32[680,128]{1,0:T(8,128)S(1)} %multiply_add_fusion.12), channel_id=1, source_target_pairs={{0,9},{1,8},{2,11},{3,10},{4,13},{5,12},{6,15},{7,14},{8,1},{9,0},... | collective-permute-start | bytes 1044488 | tf_op jit(solution)/shard_map/ppermute | solution.py:286
  75.4 11.8 %collective-permute-start.41 = (f32[85,8,128]{2,1,0:T(8,128)S(1)}, f32[85,8,128]{2,1,0:T(8,128)S(1)}, u32[]{:S(2)}, u32[]{:S(2)}) collective-permute-start(f32[85,8,128]{2,1,0:T(8,128)S(1)} %multiply_add_fusion.8), channel_id=1, source_target_pairs={{0,6},{1,7},{2,4},{3,5},{4,2},{5,3},{6,0},{7,1},{8,14},{9,15},{10,... | collective-permute-start | bytes 1044488 | tf_op jit(solution)/shard_map/ppermute | solution.py:286
  79.6 14.7 %collective-permute-start.6 = (f32[43,16,128]{2,1,0:T(8,128)S(1)}, f32[43,16,128]{2,1,0:T(8,128)S(1)}, u32[]{:S(2)}, u32[]{:S(2)}) collective-permute-start(f32[43,16,128]{2,1,0:T(8,128)S(1)} %multiply_add_fusion.4), channel_id=1, source_target_pairs={{0,9},{1,8},{2,11},{3,10},{4,13},{5,12},{6,15},{7,14},{8,1},{9,0},... | collective-permute-start | bytes 1056776 | tf_op jit(solution)/shard_map/ppermute | solution.py:286
  79.8 12.4 %collective-permute-start.27 = (f32[688,128]{1,0:T(8,128)S(1)}, f32[688,128]{1,0:T(8,128)S(1)}, u32[]{:S(2)}, u32[]{:S(2)}) collective-permute-start(f32[688,128]{1,0:T(8,128)S(1)} %multiply_add_fusion), channel_id=1, source_target_pairs={{0,96},{1,97},{2,98},{3,99},{4,100},{5,101},{6,102},{7,103},{8,104... | collective-permute-start | bytes 1056776 | tf_op jit(solution)/shard_map/ppermute | solution.py:286
  (18 other events, 128.6 us)
